TPU v7x, 32 devices: a whole 2x2x4 slice. The times are simulated.
32 devices in a mesh: dp: 16 (over z, x, core), emb: 2 (over y).
Axes of the slice: x: 2, y: 2, z: 4, core: 2. Of those that a mesh axis runs over, the one named last changes fastest.
Arguments:
- cur_ids: int32 [8192], P(('dp', 'emb')), may hold values from 0 to 3071, as said below
- prev_ids: int32 [8192], P(('dp', 'emb')), may hold values from 0 to 3071, as said below
- prev_grads: bfloat16 [8192, 128], P(('dp', 'emb')), may hold values from -6 to 6
- row_place: int32 [3072], replicated, may hold values from 0 to 3071, as said below
- table: float32 [3072, 128], P('emb'), may hold values from -6 to 6
- accum: float32 [3072, 128], P('emb'), may hold values from 0.05 to 2
- labels: float32 [8192], P('dp'), may hold values from 0 to 1
- gain: float32 [128], replicated, may hold values from 0.5 to 1.5
- w_gate: bfloat16 [128, 4096], P(None, 'emb'), may hold values from -0.5 to 0.5
- w_up: bfloat16 [128, 4096], P(None, 'emb'), may hold values from -0.5 to 0.5
- w_out: bfloat16 [4096], P('emb'), may hold values from -0.09375 to 0.09375
Outputs:
- new_table: float32 [3072, 128], P('emb')
- new_accum: float32 [3072, 128], P('emb')
- grad_gate: float32 [128, 4096], P(None, 'emb')
- grad_up: float32 [128, 4096], P(None, 'emb')
- emb_grad: float32 [8192, 128], P(('dp', 'emb'))
Inputs may be any that keep to these rules, and one draw needn't show every extreme that they name: A permutation of the table rows; row i is stored on shard row_place[i] // 1536 of emb at position row_place[i] % 1536. `cur_ids`: the 256 ids of one device name rows of one shard at most 256 times, and exactly 256 times for some shard. `prev_ids`: the 256 ids of one device name rows of one shard at most 256 times, and exactly 256 times for some shard.
All inputs are finite; a program needn't handle non-finite values.
Results may differ from a plain program's by a relative error of at most 0.0069.
Values may be sent and summed in bfloat16 or wider, within the bound.
A program may use at most 64 MiB of HBM per device.

v0:
```python
import functools
import math

import jax
import jax.numpy as jnp
from jax import lax
from jax.experimental import pallas as pl
from jax.experimental.pallas import tpu as pltpu
from jax.sharding import PartitionSpec as P

loss_weight = 64.0
learn_rate = 0.1
norm_eps = 1e-06
MESH = pl.DeviceIdType.MESH
F32 = jnp.float32
BF16 = jnp.bfloat16


def dot(a, b):
    return jnp.dot(a, b, preferred_element_type=F32)


def dot_nt(a, b):
    return lax.dot_general(a, b, (((1,), (1,)), ((), ())), preferred_element_type=F32)


def tower_kernel(
    n_dp,
    n_emb,
    scale,
    cur_ref,
    prev_ref,
    grads_ref,
    place_ref,
    table_ref,
    labels_ref,
    gain_ref,
    wg_ref,
    wu_ref,
    wo_ref,
    total_ref,
    gate_ref,
    up_ref,
    emb_ref,
    table16,
    posall,
    gall,
    contrib,
    lbuf,
    values,
    normed,
    normed_t,
    act,
    logit,
    logit_in,
    slopes,
    bn,
    bn_in,
    tpart,
    tpair,
    tsum,
    tx_in,
    tz_out,
    tz_in,
    tall,
    gpart,
    gpair,
    gsum,
    gx_in,
    gz_out,
    gz_in,
    gtotal,
    e_send,
    e_recv,
    t_send,
    t_recv,
    g_send,
    g_recv,
):
    me_dp = lax.axis_index("dp")
    me_emb = lax.axis_index("emb")
    n_chip = n_dp // 2
    n_hi = n_chip // 2
    chip = me_dp // 2
    low = chip % 2
    high = chip // 2
    par = me_dp % 2
    other = 1 - par
    partner = me_dp + 1 - 2 * par
    beside = me_dp + 2 - 4 * low
    tok = grads_ref.shape[0]
    rows = table_ref.shape[0]
    hid = wg_ref.shape[1]
    ht = 256

    def copy(src, dst, send, recv, dp, emb):
        return pltpu.make_async_remote_copy(
            src_ref=src,
            dst_ref=dst,
            send_sem=send,
            recv_sem=recv,
            device_id=(dp, emb),
            device_id_type=MESH,
        )

    emb_peers = [lax.rem(me_emb + k, n_emb) for k in range(1, n_emb)]
    ahead = [lax.rem(high + k, n_hi) for k in range(n_hi)]
    behind = [lax.rem(high + n_hi - k, n_hi) for k in range(n_hi)]
    far_peers = [(2 * h + low) * 2 + par for h in ahead]
    pending = []

    class Reduce:

        def __init__(self, part, pair, acc, x_in, z_out, z_in, full, send, recv, align):
            self.part, self.pair, self.acc, self.x_in = part, pair, acc, x_in
            self.z_out, self.z_in, self.full = z_out, z_in, full
            self.send, self.recv, self.align = send, recv, align
            self.half = pair.shape[0]
            self.size = self.half // n_chip

        def rows(self, at, size):
            return pl.ds(pl.multiple_of(at, self.align), size)

        def piece(self, lo, hi):
            return self.rows((lo * n_hi + hi) * self.size, self.size)

        def place(self, lo, hi):
            return self.rows(par * self.half + (lo * n_hi + hi) * self.size, self.size)

        def go(self, src, dst, stage, k, dp):
            one = copy(src, dst, self.send.at[stage, k], self.recv.at[stage, k], dp, me_emb)
            one.start()
            pending.append(one)
            return one

        def start(self):
            away = self.rows(other * self.half, self.half)
            self.first = self.go(self.part.at[away], self.pair, 0, 0, partner)

        def stage_x(self):
            self.first.wait_recv()
            kept = self.part[self.rows(par * self.half, self.half), :]
            joined = kept.astype(F32) + self.pair[...].astype(F32)
            self.acc[...] = joined.astype(self.acc.dtype)
            self.x = {}
            for k in list(range(1, n_hi)) + [0]:
                self.x[k] = self.go(
                    self.acc.at[self.piece(1 - low, ahead[k])], self.x_in.at[k], 1, k, beside
                )

        def joined(self, k):
            self.x[k].wait_recv()
            kept = self.acc[self.piece(low, ahead[k]), :].astype(F32)
            return kept + self.x_in[k].astype(F32)

        def stage_z(self):
            self.z = []
            for k in range(1, n_hi):
                self.z_out[k - 1] = self.joined(k).astype(self.z_out.dtype)
                self.z.append(
                    self.go(self.z_out.at[k - 1], self.z_in.at[k - 1], 2, k, far_peers[k])
                )

        def stage_sum(self):
            total = self.joined(0)
            for k, one in enumerate(self.z):
                one.wait_recv()
                total = total + self.z_in[k].astype(F32)
            mine = self.place(low, high)
            self.full[mine, :] = total.astype(self.full.dtype)
            view = self.full.at[mine]
            self.far = [self.go(view, view, 3, k, far_peers[k]) for k in range(1, n_hi)]
            self.near = [self.go(view, view, 4, 0, beside)]
            self.last = [self.go(view, view, 5, 0, partner)]

        def spread_z(self):
            for k in range(1, n_hi):
                self.far[k - 1].wait_recv()
                view = self.full.at[self.place(low, behind[k])]
                self.near.append(self.go(view, view, 4, k, beside))
                self.last.append(self.go(view, view, 5, k, partner))

        def spread_x(self):
            for k in range(n_hi):
                self.near[k].wait_recv()
                view = self.full.at[self.place(1 - low, behind[k])]
                self.last.append(self.go(view, view, 5, n_hi + k, partner))

        def finish(self):
            for one in self.last:
                one.wait_recv()

    sums = Reduce(tpart, tpair, tsum, tx_in, tz_out, tz_in, tall, t_send, t_recv, 8)
    tower = Reduce(gpart, gpair, gsum, gx_in, gz_out, gz_in, gtotal, g_send, g_recv, 16)

    barrier = pltpu.get_barrier_semaphore()
    for peer in emb_peers:
        pl.semaphore_signal(barrier, inc=1, device_id=(me_dp, peer), device_id_type=MESH)
    for peer in far_peers[1:] + [beside]:
        pl.semaphore_signal(barrier, inc=1, device_id=(peer, me_emb), device_id_type=MESH)
    pl.semaphore_signal(barrier, inc=1, device_id=(partner, me_emb), device_id_type=MESH)

    ids = jnp.concatenate([cur_ref[...], prev_ref[...]], axis=1)
    step = 512

    def place_step(i, acc):
        at = pl.multiple_of(i * step, step)
        part = place_ref[:, pl.ds(at, step)]
        both = jnp.broadcast_to(part, (8, step))
        lane_row = lax.broadcasted_iota(jnp.int32, (8, step), 0)
        halves = jnp.where(lane_row == 0, both >> 6, both & 63).astype(F32).astype(BF16)
        index = lax.broadcasted_iota(jnp.int32, (step, 2 * tok), 0) + at
        hot = jnp.where(index == ids, 1.0, 0.0).astype(BF16)
        return acc + dot(halves, hot)

    found = lax.fori_loop(
        0, place_ref.shape[1] // step, place_step, jnp.zeros((8, 2 * tok), F32)
    )
    pos = (found[0:1, :] * 64.0 + found[1:2, :]).astype(jnp.int32)
    posall[me_emb] = jnp.broadcast_to(pos, (8, 2 * tok))
    gall[me_emb] = grads_ref[...]
    table16[...] = table_ref[...].astype(BF16)
    pl.semaphore_wait(barrier, n_emb - 1 + n_hi - 1 + 2)

    first = []
    for k, peer in enumerate(emb_peers):
        one = copy(
            posall.at[me_emb], posall.at[me_emb], e_send.at[0, k], e_recv.at[0, k], me_dp, peer
        )
        one.start()
        first.append(one)
    second = []
    for k, peer in enumerate(emb_peers):
        one = copy(grads_ref, gall.at[me_emb], e_send.at[1, k], e_recv.at[1, k], me_dp, peer)
        one.start()
        second.append(one)
    pending += first + second
    for one in first:
        one.wait_recv()

    base = me_emb * rows
    kt = 256

    def lookup_step(e, carry):
        line = jnp.broadcast_to(posall[e][0:1, 0:tok] - base, (128, tok)).T
        line = jnp.concatenate([line] * (kt // 128), axis=1)
        acc = jnp.zeros((tok, 128), F32)
        for i in range(rows // kt):
            index = lax.broadcasted_iota(jnp.int32, (tok, kt), 1) + i * kt
            hot = jnp.where(index == line, 1.0, 0.0).astype(BF16)
            acc = acc + dot(hot, table16[i * kt : (i + 1) * kt, :])
        contrib[pl.ds(pl.multiple_of(e * tok, tok), tok), :] = acc.astype(BF16)
        return carry

    lax.fori_loop(0, n_emb, lookup_step, 0)
    third = []
    for k, peer in enumerate(emb_peers):
        one = copy(contrib, lbuf.at[k], e_send.at[2, k], e_recv.at[2, k], me_dp, peer)
        one.start()
        third.append(one)
    pending += third

    for one in second:
        one.wait_recv()
    half_rows = rows // 2
    pt = 128 if half_rows % 128 == 0 else half_rows

    def grad_step(i, carry):
        at = pl.multiple_of(i * pt, pt)
        index = lax.broadcasted_iota(jnp.int32, (pt, tok), 0) + (at + base)
        acc = jnp.zeros((pt, 128), F32)
        for e in range(n_emb):
            hot = jnp.where(index == posall[e][0:1, tok : 2 * tok], 1.0, 0.0).astype(BF16)
            acc = acc + dot(hot, gall[e])
        tpart[pl.ds(at, pt), :] = acc
        return carry

    lax.fori_loop(0, rows // pt, grad_step, 0)
    sums.start()
    sums.stage_x()

    for one in third:
        one.wait_recv()
    looked = contrib[...].astype(F32)
    for k in range(n_emb - 1):
        looked = looked + lbuf[k].astype(F32)
    values[...] = looked
    inverse_rms = lax.rsqrt(jnp.mean(looked * looked, axis=1, keepdims=True) + norm_eps)
    norm16 = (looked * inverse_rms * gain_ref[...]).astype(BF16)
    normed[...] = norm16
    normed_t[...] = norm16.astype(F32).T

    logit[...] = jnp.zeros_like(logit)

    def tower_step(j, carry):
        cols = pl.ds(pl.multiple_of(j * ht, ht), ht)
        gate = dot(normed[...], wg_ref[:, cols])
        up = dot(normed[...], wu_ref[:, cols])
        sig = jax.nn.sigmoid(gate)
        activated = gate * sig
        act[0, :, cols] = (up * (sig + activated * (1.0 - sig))).astype(BF16)
        act[1, :, cols] = activated.astype(BF16)
        hidden = (activated * up).astype(BF16)
        head = jnp.broadcast_to(wo_ref[:, cols].astype(F32), (8, ht)).astype(BF16)
        logit[...] += dot_nt(head, hidden)
        return carry

    tiles = hid // ht
    some = max(1, 5 * tiles // 8)
    lax.fori_loop(0, some, tower_step, 0)
    sums.stage_z()
    lax.fori_loop(some, tiles, tower_step, 0)
    fourth = []
    for k, peer in enumerate(emb_peers):
        one = copy(logit, logit_in.at[k], e_send.at[3, k], e_recv.at[3, k], me_dp, peer)
        one.start()
        fourth.append(one)
    pending += fourth

    bn[...] = jnp.zeros_like(bn)

    def back_step(j, carry):
        cols = pl.ds(pl.multiple_of(j * ht, ht), ht)
        head = wo_ref[:, cols].astype(F32)
        wg = (wg_ref[:, cols].astype(F32) * head).astype(BF16)
        wu = (wu_ref[:, cols].astype(F32) * head).astype(BF16)
        bn[...] += dot_nt(act[0, :, cols], wg) + dot_nt(act[1, :, cols], wu)
        return carry

    lax.fori_loop(0, hid // ht, back_step, 0)
    fifth = []
    for k, peer in enumerate(emb_peers):
        one = copy(
            bn.at[pl.ds(pl.multiple_of(peer * tok, tok), tok)],
            bn_in.at[k],
            e_send.at[4, k],
            e_recv.at[4, k],
            me_dp,
            peer,
        )
        one.start()
        fifth.append(one)
    pending += fifth

    for one in fourth:
        one.wait_recv()
    logits = logit[...]
    for k in range(n_emb - 1):
        logits = logits + logit_in[k]
    slope = loss_weight * (jax.nn.sigmoid(logits) - labels_ref[...])
    slopes[...] = slope
    lead = (normed_t[...] * slope[0:1, :]).astype(BF16)

    def weight_grads(which):
        for j in range(hid // ht):
            cols = slice(j * ht, (j + 1) * ht)
            head = wo_ref[:, cols].astype(F32) * scale
            part = (dot(lead, act[which, :, cols]) * head).astype(BF16)
            for b in range(ht // 128):
                at = j * ht + b * 128
                gpart[pl.ds(pl.multiple_of(which * hid + at, 128), 128), :] = part[:, b * 128 : (b + 1) * 128]

    weight_grads(other)
    tower.start()
    sums.stage_sum()
    weight_grads(par)
    tower.stage_x()

    for one in fifth:
        one.wait_recv()
    own = pl.ds(pl.multiple_of(me_emb * tok, tok), tok)
    back = bn[own, :]
    for k in range(n_emb - 1):
        back = back + bn_in[k]
    slope_col = jnp.broadcast_to(slopes[0:1, own], (128, tok)).T
    scaled = back * slope_col * gain_ref[...]
    x = values[own, :]
    inv = lax.rsqrt(jnp.mean(x * x, axis=1, keepdims=True) + norm_eps)
    emb_ref[...] = inv * scaled - x * (inv * inv * inv) * jnp.mean(
        x * scaled, axis=1, keepdims=True
    )

    tower.stage_z()
    sums.spread_z()
    tower.stage_sum()
    sums.spread_x()
    tower.spread_z()
    tower.spread_x()
    sums.finish()
    total_ref[...] = tall[...]
    tower.finish()
    for b in range(hid // 128):
        cols = slice(b * 128, (b + 1) * 128)
        gate_ref[:, cols] = gtotal[cols, :]
        up_ref[:, cols] = gtotal[hid + b * 128 : hid + (b + 1) * 128, :]
    for one in pending:
        one.wait_send()


def on_device(
    cur_ids, prev_ids, prev_grads, row_place, table, accum, labels, gain, w_gate, w_up, w_out
):
    n_emb = lax.axis_size("emb")
    n_dp = lax.axis_size("dp")
    n_chip = n_dp // 2
    n_hi = n_chip // 2
    rows, width = table.shape
    tok = cur_ids.shape[0]
    group = tok * n_emb
    hid = w_gate.shape[1]
    scale = 1.0 / math.sqrt(tok * n_emb * n_dp)
    vmem = pl.BlockSpec(memory_space=pltpu.VMEM)
    n_peer = max(n_emb - 1, 1)
    dma = pltpu.SemaphoreType.DMA
    total, gate, up, emb_grad = pl.pallas_call(
        functools.partial(tower_kernel, n_dp, n_emb, scale),
        out_shape=(
            jax.ShapeDtypeStruct((rows, width), F32),
            jax.ShapeDtypeStruct((width, hid), BF16),
            jax.ShapeDtypeStruct((width, hid), BF16),
            jax.ShapeDtypeStruct((tok, width), F32),
        ),
        in_specs=[vmem] * 10,
        out_specs=(vmem,) * 4,
        scratch_shapes=[
            pltpu.VMEM((rows, width), BF16),
            pltpu.VMEM((n_emb, 8, 2 * tok), jnp.int32),
            pltpu.VMEM((n_emb, tok, width), BF16),
            pltpu.VMEM((group, width), BF16),
            pltpu.VMEM((n_peer, group, width), BF16),
            pltpu.VMEM((group, width), F32),
            pltpu.VMEM((group, width), BF16),
            pltpu.VMEM((width, group), F32),
            pltpu.VMEM((2, group, hid), BF16),
            pltpu.VMEM((8, group), F32),
            pltpu.VMEM((n_peer, 8, group), F32),
            pltpu.VMEM((8, group), F32),
            pltpu.VMEM((group, width), F32),
            pltpu.VMEM((n_peer, tok, width), F32),
            pltpu.VMEM((rows, width), F32),
            pltpu.VMEM((rows // 2, width), F32),
            pltpu.VMEM((rows // 2, width), F32),
            pltpu.VMEM((n_hi, rows // n_dp, width), F32),
            pltpu.VMEM((n_hi - 1, rows // n_dp, width), F32),
            pltpu.VMEM((n_hi - 1, rows // n_dp, width), F32),
            pltpu.VMEM((rows, width), F32),
            pltpu.VMEM((2 * hid, width), BF16),
            pltpu.VMEM((hid, width), BF16),
            pltpu.VMEM((hid, width), BF16),
            pltpu.VMEM((n_hi, hid // n_chip, width), BF16),
            pltpu.VMEM((n_hi - 1, hid // n_chip, width), BF16),
            pltpu.VMEM((n_hi - 1, hid // n_chip, width), BF16),
            pltpu.VMEM((2 * hid, width), BF16),
            dma((5, n_peer)),
            dma((5, n_peer)),
            dma((6, 2 * n_hi)),
            dma((6, 2 * n_hi)),
            dma((6, 2 * n_hi)),
            dma((6, 2 * n_hi)),
        ],
        compiler_params=pltpu.CompilerParams(
            collective_id=0, has_side_effects=True, vmem_limit_bytes=60 * 1024 * 1024
        ),
    )(
        cur_ids.reshape(1, -1),
        prev_ids.reshape(1, -1),
        prev_grads,
        row_place.reshape(1, -1),
        table,
        labels.reshape(1, -1),
        gain.reshape(1, -1),
        w_gate,
        w_up,
        w_out.reshape(1, -1),
    )
    new_accum = accum + total * total
    new_table = table - learn_rate * total * lax.rsqrt(new_accum)
    return (new_table, new_accum, gate.astype(F32), up.astype(F32), emb_grad)


def solution(mesh):
    placed = (
        P(("dp", "emb")),
        P(("dp", "emb")),
        P(("dp", "emb"), None),
        P(),
        P("emb", None),
        P("emb", None),
        P("dp"),
        P(),
        P(None, "emb"),
        P(None, "emb"),
        P("emb"),
    )
    return jax.shard_map(
        on_device,
        mesh=mesh,
        in_specs=placed,
        out_specs=(
            P("emb", None),
            P("emb", None),
            P(None, "emb"),
            P(None, "emb"),
            P(("dp", "emb"), None),
        ),
        check_vma=False,
    )
```

profile of v0, /device:TPU:0, one launch (start us, length us, event | category | flops | bytes accessed | tf_op | source)
XLA Modules:
  0.0 56.9 jit_solution(8765689456496155141)
XLA Ops:
  0.6 0.0 copy-start.5
  0.6 0.7 %copy-done.5 = bf16[2048]{0:T(1024)(128)(2,1)S(1)} copy-done((bf16[2048]{0:T(1024)(128)(2,1)S(1)}, bf16[2048]{0:T(1024)(128)(2,1)}, u32[]{:S(2)}) %copy-start.5) | copy-done | bytes 4120
  1.3 0.6 %reshape.33.wo_ref = bf16[1,2048]{1,0:T(2,128)(2,1)} reshape(bf16[2048]{0:T(1024)(128)(2,1)S(1)} %copy-done.5) | data formatting | bytes 8192 | tf_op jit(solution)/shard_map/reshape | solution.py:474
  1.9 0.0 copy-start
  1.9 0.0 copy-start.1
  1.9 49.6 %shard_map.146 = (f32[1536,128]{1,0:T(8,128)}, bf16[128,2048]{1,0:T(8,128)(2,1)}, bf16[128,2048]{1,0:T(8,128)(2,1)}, f32[256,128]{1,0:T(8,128)}) custom-call(s32[1,256]{1,0:T(1,128)} %bitcast.7, s32[1,256]{1,0:T(1,128)} %bitcast.8, bf16[256,128]{1,0:T(8,128)(2,1)} %grads_ref.1, s32[1,3072]{1,0:T(1,128)} %bitcast.5, f32[1536,128]{1,0:T(8,128)} %table_ref.1, ...), custom_call_target="tpu_custom_call" | custom-call | tf_op jit(solution)/shard_map/pallas_call | solution.py:415
  51.5 0.0 copy-done
  51.5 0.0 copy-done.1
  51.6 0.0 copy-start.3
  51.6 2.5 %multiply_subtract_fusion = (f32[1536,128]{1,0:T(8,128)}, f32[1536,128]{1,0:T(8,128)}) fusion(f32[1536,128]{1,0:T(8,128)S(1)} %copy-done, f32[1536,128]{1,0:T(8,128)} %get-tuple-element.9, f32[1536,128]{1,0:T(8,128)S(1)} %copy-done.1), kind=kLoop, calls=%fused_computation | loop fusion | flops 983040 | bytes 3932160 | tf_op jit(solution)/shard_map/sub | solution.py:477
  54.0 0.0 copy-done.3
  54.0 0.0 copy-start.2
  54.1 1.1 %convert_element_type.6 = f32[128,2048]{1,0:T(8,128)} convert(bf16[128,2048]{1,0:T(8,128)(2,1)S(1)} %copy-done.3) | non-fusion elementwise | flops 262144 | bytes 1572864 | tf_op jit(solution)/shard_map/convert_element_type | solution.py:478
  55.1 0.1 copy-done.2
  55.2 0.0 copy-start.4
  55.2 1.1 %convert_element_type.7 = f32[128,2048]{1,0:T(8,128)} convert(bf16[128,2048]{1,0:T(8,128)(2,1)S(1)} %copy-done.2) | non-fusion elementwise | flops 262144 | bytes 1572864 | tf_op jit(solution)/shard_map/convert_element_type | solution.py:478
  56.3 0.0 copy-done.4
  56.3 0.7 %copy.17 = f32[256,128]{1,0:T(8,128)} copy(f32[256,128]{1,0:T(8,128)S(1)} %copy-done.4) | data formatting | bytes 262144
Async XLA Ops:
  0.6 0.7 %copy-start.5 = (bf16[2048]{0:T(1024)(128)(2,1)S(1)}, bf16[2048]{0:T(1024)(128)(2,1)}, u32[]{:S(2)}) copy-start(bf16[2048]{0:T(1024)(128)(2,1)} %param.21) | copy-start | bytes 12292
  1.9 49.6 %copy-start = (f32[1536,128]{1,0:T(8,128)S(1)}, f32[1536,128]{1,0:T(8,128)}, u32[]{:S(2)}) copy-start(f32[1536,128]{1,0:T(8,128)} %table_ref.1) | copy-start | bytes 2359300
  1.9 49.6 %copy-start.1 = (f32[1536,128]{1,0:T(8,128)S(1)}, f32[1536,128]{1,0:T(8,128)}, u32[]{:S(2)}) copy-start(f32[1536,128]{1,0:T(8,128)} %param.16) | copy-start | bytes 2359300
  51.6 2.5 %copy-start.3 = (bf16[128,2048]{1,0:T(8,128)(2,1)S(1)}, bf16[128,2048]{1,0:T(8,128)(2,1)}, u32[]{:S(2)}) copy-start(bf16[128,2048]{1,0:T(8,128)(2,1)} %get-tuple-element.10) | copy-start | bytes 1572868
  54.0 1.1 %copy-start.2 = (bf16[128,2048]{1,0:T(8,128)(2,1)S(1)}, bf16[128,2048]{1,0:T(8,128)(2,1)}, u32[]{:S(2)}) copy-start(bf16[128,2048]{1,0:T(8,128)(2,1)} %get-tuple-element.11) | copy-start | bytes 1572868
  55.2 1.1 %copy-start.4 = (f32[256,128]{1,0:T(8,128)S(1)}, f32[256,128]{1,0:T(8,128)}, u32[]{:S(2)}) copy-start(f32[256,128]{1,0:T(8,128)} %get-tuple-element.24) | copy-start | bytes 393220
where the time goes:
time: 57.4 us; the launch traced here: 56.9 us
  Pallas kernels  49.6 us (86%)
  other arithmetic  4.62 us (8%)
  local copies, waits for them, and re-layouts  2.02 us (4%)
  between operations  0.68 us (1%)
    pallas_call x1, Pallas kernels, on_device(): pl.pallas_call(functools.partial(tower_kernel, n_dp, n_emb, scale), out_s...  49.6 us
    sub x1, other arithmetic, on_device(): new_table = table - learn_rate * total * lax.rsqrt(new_accum)  2.48 us
    convert_element_type x2, other arithmetic, on_device(): return (new_table, new_accum, gate.astype(F32), up.astype(F32), emb_grad)  2.14 us
    unnamed x13, local copies, waits for them, and re-layouts  1.41 us

commit v1 on v0

v1 whole, which is shorter than its diff:
```python
import functools
import math

import jax
import jax.numpy as jnp
from jax import lax
from jax.experimental import pallas as pl
from jax.experimental.pallas import tpu as pltpu
from jax.sharding import PartitionSpec as P

loss_weight = 64.0
learn_rate = 0.1
norm_eps = 1e-06
MESH = pl.DeviceIdType.MESH
F32 = jnp.float32
BF16 = jnp.bfloat16
LANES = 128


def dot(a, b):
    return jnp.dot(a, b, preferred_element_type=F32)


def dot_nt(a, b):
    return lax.dot_general(a, b, (((1,), (1,)), ((), ())), preferred_element_type=F32)


class Reduce:
    def __init__(self, at, copy, pending, bufs, send, recv):
        self.at, self.copy, self.pending = at, copy, pending
        self.part, self.pair, self.x_out, self.keep, self.x_in, self.z_out, self.z_in, self.full = bufs
        self.send, self.recv = send, recv
        self.half = self.pair.shape[0]
        self.quarter = self.half // 2
        self.size = self.quarter // at["n_hi"]

    def rows(self, start, size):
        return pl.ds(pl.multiple_of(start, math.gcd(size, 128)), size)

    def place(self, lo, hi):
        return self.rows(self.at["par"] * self.half + lo * self.quarter + hi * self.size, self.size)

    def go(self, src, dst, stage, k, dp):
        one = self.copy(src, dst, self.send.at[stage, k], self.recv.at[stage, k], dp, self.at["emb"])
        one.start()
        self.pending.append(one)
        return one

    def start(self, away):
        lo = 1 - self.at["low"] if away else self.at["low"]
        src = self.rows((1 - self.at["par"]) * self.half + lo * self.quarter, self.quarter)
        dst = self.rows(lo * self.quarter, self.quarter)
        one = self.go(self.part.at[src], self.pair.at[dst], 0, 0 if away else 1, self.at["partner"])
        if away:
            self.first_away = one
        else:
            self.first_keep = one

    def stage_x(self):
        at = self.at
        self.first_away.wait_recv()
        self.x = {}
        lo = (1 - at["low"]) * self.quarter
        for k in list(range(1, at["n_hi"])) + [0]:
            piece = at["ahead"][k] * self.size
            mine = self.part[self.rows(at["par"] * self.half + lo + piece, self.size), :]
            theirs = self.pair[self.rows(lo + piece, self.size), :]
            self.x_out[k] = (mine.astype(F32) + theirs.astype(F32)).astype(BF16)
            self.x[k] = self.go(self.x_out.at[k], self.x_in.at[k], 1, k, at["beside"])

    def stage_keep(self):
        at = self.at
        self.first_keep.wait_recv()
        lo = at["low"] * self.quarter
        mine = self.part[self.rows(at["par"] * self.half + lo, self.quarter), :]
        theirs = self.pair[self.rows(lo, self.quarter), :]
        self.keep[...] = mine.astype(F32) + theirs.astype(F32)

    def joined(self, k):
        self.x[k].wait_recv()
        kept = self.keep[self.rows(self.at["ahead"][k] * self.size, self.size), :]
        return kept + self.x_in[k].astype(F32)

    def stage_z(self):
        self.z = []
        for k in range(1, self.at["n_hi"]):
            self.z_out[k - 1] = self.joined(k).astype(BF16)
            self.z.append(
                self.go(self.z_out.at[k - 1], self.z_in.at[k - 1], 2, k, self.at["far"][k])
            )

    def stage_sum(self):
        at = self.at
        total = self.joined(0)
        for k, one in enumerate(self.z):
            one.wait_recv()
            total = total + self.z_in[k].astype(F32)
        mine = self.place(at["low"], at["high"])
        self.full[mine, :] = total.astype(BF16)
        view = self.full.at[mine]
        self.spread = [self.go(view, view, 3, k, at["far"][k]) for k in range(1, at["n_hi"])]
        self.near = [self.go(view, view, 4, 0, at["beside"])]
        self.last = [self.go(view, view, 5, 0, at["partner"])]

    def spread_z(self):
        at = self.at
        for k in range(1, at["n_hi"]):
            self.spread[k - 1].wait_recv()
            view = self.full.at[self.place(at["low"], at["behind"][k])]
            self.near.append(self.go(view, view, 4, k, at["beside"]))
            self.last.append(self.go(view, view, 5, k, at["partner"]))

    def spread_x(self):
        at = self.at
        n_hi = at["n_hi"]
        for k in range(n_hi):
            self.near[k].wait_recv()
            view = self.full.at[self.place(1 - at["low"], at["behind"][k])]
            self.last.append(self.go(view, view, 5, n_hi + k, at["partner"]))

    def finish(self):
        for one in self.last:
            one.wait_recv()


def tower_kernel(
    n_dp,
    n_emb,
    scale,
    cur_ref,
    prev_ref,
    grads_ref,
    place_ref,
    table_ref,
    labels_ref,
    gain_ref,
    wg_ref,
    wu_ref,
    wo_ref,
    total_ref,
    tower_ref,
    emb_ref,
    ids,
    gall,
    place,
    table,
    labels,
    gain,
    wg,
    wu,
    wo,
    table16,
    wo_row,
    scaled_w,
    contrib,
    lbuf,
    values,
    normed,
    normed_t,
    act,
    logit_acc,
    logit,
    logit_in,
    slopes,
    lead,
    bn,
    bn_in,
    tpart,
    tpair,
    tx_out,
    tkeep,
    tx_in,
    tz_out,
    tz_in,
    tall,
    gpart,
    gpair,
    gx_out,
    gkeep,
    gx_in,
    gz_out,
    gz_in,
    gall_sum,
    load,
    e_send,
    e_recv,
    t_send,
    t_recv,
    g_send,
    g_recv,
):
    me_dp = lax.axis_index("dp")
    me_emb = lax.axis_index("emb")
    n_chip = n_dp // 2
    n_hi = n_chip // 2
    chip = me_dp // 2
    low = chip % 2
    high = chip // 2
    par = me_dp % 2
    partner = me_dp + 1 - 2 * par
    beside = me_dp + 2 - 4 * low
    tok = gall.shape[1]
    rows = table.shape[0]
    hid = wg.shape[1]
    ht = 256
    tiles = hid // ht

    def copy(src, dst, send, recv, dp, emb):
        return pltpu.make_async_remote_copy(
            src_ref=src,
            dst_ref=dst,
            send_sem=send,
            recv_sem=recv,
            device_id=(dp, emb),
            device_id_type=MESH,
        )

    def other_emb(k):
        return lax.rem(me_emb + k, n_emb)

    def tokens(e):
        return pl.ds(pl.multiple_of(e * tok, tok), tok)

    ahead = [lax.rem(high + k, n_hi) for k in range(n_hi)]
    behind = [lax.rem(high + n_hi - k, n_hi) for k in range(n_hi)]
    far = [(2 * h + low) * 2 + par for h in ahead]
    at = dict(
        n_hi=n_hi, par=par, low=low, high=high, partner=partner, beside=beside,
        ahead=ahead, behind=behind, far=far, emb=me_emb,
    )
    pending = []
    sums = Reduce(
        at, copy, pending, (tpart, tpair, tx_out, tkeep, tx_in, tz_out, tz_in, tall), t_send, t_recv
    )
    tower = Reduce(
        at, copy, pending, (gpart, gpair, gx_out, gkeep, gx_in, gz_out, gz_in, gall_sum), g_send, g_recv
    )

    barrier = pltpu.get_barrier_semaphore()
    for k in range(1, n_emb):
        pl.semaphore_signal(barrier, inc=1, device_id=(me_dp, other_emb(k)), device_id_type=MESH)
    for peer in far[1:] + [beside, partner]:
        pl.semaphore_signal(barrier, inc=1, device_id=(peer, me_emb), device_id_type=MESH)

    loads = []
    for i, (src, dst) in enumerate(
        [
            (cur_ref, ids.at[me_emb, 0]),
            (prev_ref, ids.at[me_emb, 1]),
            (place_ref, place),
            (grads_ref, gall.at[me_emb]),
            (table_ref, table),
            (wo_ref, wo),
            (wg_ref, wg),
            (wu_ref, wu),
            (gain_ref, gain),
            (labels_ref, labels),
        ]
    ):
        one = pltpu.make_async_copy(src, dst, load.at[i])
        one.start()
        loads.append(one)
    loads[0].wait()
    loads[1].wait()
    pl.semaphore_wait(barrier, n_emb - 1 + n_hi - 1 + 2)

    def to_peers(src, dst_of, stage, slot, peers=None):
        sent = []
        for k in peers or range(1, n_emb):
            one = copy(
                src(k), dst_of(k), e_send.at[stage, slot, k - 1], e_recv.at[stage, slot, k - 1], me_dp, other_emb(k)
            )
            one.start()
            sent.append(one)
        pending.extend(sent)
        return sent

    own_ids = ids.at[me_emb]
    id_copies = to_peers(lambda k: own_ids, lambda k: own_ids, 0, 0)
    loads[3].wait()
    own_grads = gall.at[me_emb]
    grad_copies = to_peers(lambda k: own_grads, lambda k: own_grads, 1, 0)

    loads[2].wait()
    groups = place.shape[0]
    stored = place[...]
    digits = jnp.concatenate([stored >> 6, stored & 63], axis=0).astype(F32).astype(BF16)

    def place_of(wanted):
        lane = lax.broadcasted_iota(jnp.int32, (LANES, tok), 0)
        hot = jnp.where(lane == (wanted & (LANES - 1)), 1.0, 0.0).astype(BF16)
        found = dot(digits, hot)
        found = found[0:groups, :] * 64.0 + found[groups : 2 * groups, :]
        group = lax.broadcasted_iota(jnp.int32, (groups, tok), 0)
        picked = jnp.where(group == (wanted >> 7), found, 0.0)
        return jnp.sum(picked, axis=0, keepdims=True).astype(jnp.int32)

    base = me_emb * rows
    kt = 256
    prev_pos = []

    loads[4].wait()
    table16[...] = table[...].astype(BF16)

    row_copies = {}
    for s in range(n_emb):
        e = other_emb(s)
        if s > 0:
            id_copies[n_emb - s - 1].wait_recv()
        line = jnp.broadcast_to(place_of(ids[e, 0]) - base, (LANES, tok)).T
        line = jnp.concatenate([line] * (kt // LANES), axis=1)
        acc = jnp.zeros((tok, LANES), F32)
        for i in range(rows // kt):
            index = lax.broadcasted_iota(jnp.int32, (tok, kt), 1) + i * kt
            hot = jnp.where(index == line, 1.0, 0.0).astype(BF16)
            acc = acc + dot(hot, table16[i * kt : (i + 1) * kt, :])
        view = contrib.at[tokens(e)]
        contrib[tokens(e), :] = acc.astype(BF16)
        for k, one in zip(
            range(1, n_emb), to_peers(lambda k: view, lambda k: lbuf.at[k - 1, tokens(e)], 2, s)
        ):
            row_copies[k, s] = one
        prev_pos.append((e, place_of(ids[e, 1]) - base))

    for one in grad_copies:
        one.wait_recv()
    half_rows = rows // 2
    pt = 128 if half_rows % 128 == 0 else half_rows

    def grad_half(which):
        def grad_step(i, carry):
            at_row = pl.multiple_of(which * half_rows + i * pt, pt)
            index = lax.broadcasted_iota(jnp.int32, (pt, tok), 0) + at_row
            acc = jnp.zeros((pt, LANES), F32)
            for e, pos in prev_pos:
                hot = jnp.where(index == pos, 1.0, 0.0).astype(BF16)
                acc = acc + dot(hot, gall[e])
            tpart[pl.ds(at_row, pt), :] = acc
            return carry

        lax.fori_loop(0, half_rows // pt, grad_step, 0)

    grad_half(1 - par)
    sums.start(True)
    sums.start(False)
    grad_half(par)
    for one in loads[5:]:
        one.wait()
    wo_row[...] = wo[...].astype(F32)
    per_tile = ht // LANES

    def head_of(j):
        parts = [wo_row[pl.ds(j * per_tile + b, 1), :] for b in range(per_tile)]
        return jnp.concatenate(parts, axis=1)

    sums.stage_x()

    def scale_step(j, carry):
        cols = pl.ds(pl.multiple_of(j * ht, ht), ht)
        head = head_of(j)
        scaled_w[0, :, cols] = (wg[:, cols].astype(F32) * head).astype(BF16)
        scaled_w[1, :, cols] = (wu[:, cols].astype(F32) * head).astype(BF16)
        return carry

    lax.fori_loop(0, tiles, scale_step, 0)
    sums.stage_keep()

    def forward(e):
        span = tokens(e)
        looked = contrib[span, :].astype(F32)
        for k in range(1, n_emb):
            looked = looked + lbuf[k - 1, span, :].astype(F32)
        values[span, :] = looked
        inverse_rms = lax.rsqrt(jnp.mean(looked * looked, axis=1, keepdims=True) + norm_eps)
        norm = (looked * inverse_rms * gain[...]).astype(BF16)
        normed[span, :] = norm
        normed_t[:, span] = norm.astype(F32).T
        logit_acc[...] = jnp.zeros_like(logit_acc)

        def tower_step(j, carry):
            cols = pl.ds(pl.multiple_of(j * ht, ht), ht)
            gate = dot(normed[span, :], wg[:, cols])
            up = dot(normed[span, :], wu[:, cols])
            sig = 0.5 + 0.5 * jnp.tanh(0.5 * gate)
            activated = gate * sig
            act[0, span, cols] = (up * (sig + activated * (1.0 - sig))).astype(BF16)
            act[1, span, cols] = activated.astype(BF16)
            weighed = activated * up * head_of(j)
            part = weighed[:, 0:LANES]
            for b in range(1, per_tile):
                part = part + weighed[:, b * LANES : (b + 1) * LANES]
            logit_acc[...] += part
            return carry

        lax.fori_loop(0, tiles, tower_step, 0)
        logit[e] = jnp.sum(logit_acc[...].T, axis=0, keepdims=True)

    def backward(e):
        span = tokens(e)

        def back_step(j, carry):
            cols = pl.ds(pl.multiple_of(j * ht, ht), ht)
            return carry + dot_nt(act[0, span, cols], scaled_w[0, :, cols]) + dot_nt(
                act[1, span, cols], scaled_w[1, :, cols]
            )

        bn[span, :] = lax.fori_loop(0, tiles, back_step, jnp.zeros((tok, LANES), F32))

    logit_copies = []
    for q in range(1, n_emb + 1):
        e = other_emb(n_emb - q)
        for k in range(1, n_emb):
            row_copies[k, (k - q) % n_emb].wait_recv()
        forward(e)
        view = logit.at[e]
        logit_copies += to_peers(lambda k: view, lambda k: logit_in.at[k - 1, e], 3, q - 1)
        if q == 1:
            sums.stage_z()
    back_copies = []
    for q in range(1, n_emb):
        e = other_emb(n_emb - q)
        backward(e)
        k = n_emb - q
        view = bn.at[tokens(e)]
        back_copies += to_peers(lambda k: view, lambda k: bn_in.at[k - 1], 4, 0, [k])
    backward(me_emb)
    sums.stage_sum()

    for one in logit_copies:
        one.wait_recv()
    for e in range(n_emb):
        logits = logit[e]
        for k in range(n_emb - 1):
            logits = logits + logit_in[k, e]
        slope = loss_weight * (jax.nn.sigmoid(logits) - labels[e])
        slopes[e] = slope
        span = slice(e * tok, (e + 1) * tok)
        lead[:, span] = (normed_t[:, span] * slope).astype(BF16)

    def weight_grads(which, lo):
        def step(i, carry):
            j = lo * (tiles // 2) + i
            cols = pl.ds(pl.multiple_of(j * ht, ht), ht)
            part = (dot(lead[...], act[which, :, cols]) * (head_of(j) * scale)).astype(BF16)
            for b in range(per_tile):
                to = which * hid + j * ht + b * LANES
                gpart[pl.ds(pl.multiple_of(to, LANES), LANES), :] = part[:, b * LANES : (b + 1) * LANES]
            return carry

        lax.fori_loop(0, tiles // 2, step, 0)

    weight_grads(1 - par, 1 - low)
    tower.start(True)
    weight_grads(par, 1 - low)
    weight_grads(1 - par, low)
    tower.start(False)
    tower.stage_x()
    weight_grads(par, low)
    tower.stage_keep()
    sums.spread_z()

    for one in back_copies:
        one.wait_recv()
    own = tokens(me_emb)
    back = bn[own, :]
    for k in range(n_emb - 1):
        back = back + bn_in[k]
    slope_col = jnp.broadcast_to(slopes[me_emb], (LANES, tok)).T
    scaled = back * slope_col * gain[...]
    x = values[own, :]
    inv = lax.rsqrt(jnp.mean(x * x, axis=1, keepdims=True) + norm_eps)
    emb_ref[...] = inv * scaled - x * (inv * inv * inv) * jnp.mean(
        x * scaled, axis=1, keepdims=True
    )

    tower.stage_z()
    sums.spread_x()
    tower.stage_sum()
    sums.finish()
    total_ref[...] = tall[...]
    tower.spread_z()
    tower.spread_x()
    tower.finish()
    tower_ref[...] = gall_sum[...]
    for one in pending:
        one.wait_send()


def write_kernel(
    total_ref, table_ref, accum_ref, tower_ref, emb_ref,
    table_out, accum_out, gate_out, up_out, emb_out,
    new_table, new_accum, gate, up, sem,
):
    hid = gate.shape[1]
    rows = new_table.shape[0]
    sent = []

    def send(src, dst):
        one = pltpu.make_async_copy(src, dst, sem.at[len(sent)])
        one.start()
        sent.append(one)

    send(emb_ref, emb_out)
    n_col = 2
    for which, (buf, out) in enumerate(((gate, gate_out), (up, up_out))):
        for c in range(n_col):
            for b in range(c * hid // LANES // n_col, (c + 1) * hid // LANES // n_col):
                start = which * hid + b * LANES
                buf[:, b * LANES : (b + 1) * LANES] = tower_ref[start : start + LANES, :].astype(F32)
            cols = slice(c * hid // n_col, (c + 1) * hid // n_col)
            send(buf.at[:, cols], out.at[:, cols])
    n_row = 2
    for c in range(n_row):
        span = slice(c * rows // n_row, (c + 1) * rows // n_row)
        total = total_ref[span, :].astype(F32)
        grown = accum_ref[span, :] + total * total
        new_accum[span, :] = grown
        new_table[span, :] = table_ref[span, :] - learn_rate * total * lax.rsqrt(grown)
        send(new_accum.at[span], accum_out.at[span])
        send(new_table.at[span], table_out.at[span])
    for one in sent:
        one.wait()


def on_device(
    cur_ids, prev_ids, prev_grads, row_place, table, accum, labels, gain, w_gate, w_up, w_out
):
    n_emb = lax.axis_size("emb")
    n_dp = lax.axis_size("dp")
    n_chip = n_dp // 2
    n_hi = n_chip // 2
    rows, width = table.shape
    tok = cur_ids.shape[0]
    group = tok * n_emb
    hid = w_gate.shape[1]
    groups = row_place.shape[0] // LANES
    scale = 1.0 / math.sqrt(tok * n_emb * n_dp)
    vmem = pl.BlockSpec(memory_space=pltpu.VMEM)
    hbm = pl.BlockSpec(memory_space=pltpu.HBM)
    n_peer = max(n_emb - 1, 1)
    dma = pltpu.SemaphoreType.DMA
    I32 = jnp.int32

    def reduce_buffers(total_rows, dtype):
        half = total_rows // 2
        size = half // n_chip
        return [
            pltpu.VMEM((total_rows, width), dtype),
            pltpu.VMEM((half, width), dtype),
            pltpu.VMEM((n_hi, size, width), BF16),
            pltpu.VMEM((half // 2, width), F32),
            pltpu.VMEM((n_hi, size, width), BF16),
            pltpu.VMEM((n_hi - 1, size, width), BF16),
            pltpu.VMEM((n_hi - 1, size, width), BF16),
            pltpu.VMEM((total_rows, width), BF16),
        ]

    total, tower, emb_grad = pl.pallas_call(
        functools.partial(tower_kernel, n_dp, n_emb, scale),
        out_shape=(
            jax.ShapeDtypeStruct((rows, width), BF16),
            jax.ShapeDtypeStruct((2 * hid, width), BF16),
            jax.ShapeDtypeStruct((tok, width), F32),
        ),
        in_specs=[hbm] * 10,
        out_specs=(vmem,) * 3,
        scratch_shapes=[
            pltpu.VMEM((n_emb, 2, 1, tok), I32),
            pltpu.VMEM((n_emb, tok, width), BF16),
            pltpu.VMEM((groups, LANES), I32),
            pltpu.VMEM((rows, width), F32),
            pltpu.VMEM((n_emb, 1, tok), F32),
            pltpu.VMEM((1, width), F32),
            pltpu.VMEM((width, hid), BF16),
            pltpu.VMEM((width, hid), BF16),
            pltpu.VMEM((hid // LANES, LANES), BF16),
            pltpu.VMEM((rows, width), BF16),
            pltpu.VMEM((hid // LANES, LANES), F32),
            pltpu.VMEM((2, width, hid), BF16),
            pltpu.VMEM((group, width), BF16),
            pltpu.VMEM((n_peer, group, width), BF16),
            pltpu.VMEM((group, width), F32),
            pltpu.VMEM((group, width), BF16),
            pltpu.VMEM((width, group), F32),
            pltpu.VMEM((2, group, hid), BF16),
            pltpu.VMEM((tok, width), F32),
            pltpu.VMEM((n_emb, 1, tok), F32),
            pltpu.VMEM((n_peer, n_emb, 1, tok), F32),
            pltpu.VMEM((n_emb, 1, tok), F32),
            pltpu.VMEM((width, group), BF16),
            pltpu.VMEM((group, width), F32),
            pltpu.VMEM((n_peer, tok, width), F32),
        ]
        + reduce_buffers(rows, F32)
        + reduce_buffers(2 * hid, BF16)
        + [
            dma((10,)),
            dma((5, n_emb, n_peer)),
            dma((5, n_emb, n_peer)),
            dma((6, 2 * n_hi)),
            dma((6, 2 * n_hi)),
            dma((6, 2 * n_hi)),
            dma((6, 2 * n_hi)),
        ],
        compiler_params=pltpu.CompilerParams(
            collective_id=0, has_side_effects=True, vmem_limit_bytes=40 * 1024 * 1024
        ),
    )(
        cur_ids.reshape(1, -1),
        prev_ids.reshape(1, -1),
        prev_grads,
        row_place.reshape(-1, LANES),
        table,
        labels.reshape(n_emb, 1, -1),
        gain.reshape(1, -1),
        w_gate,
        w_up,
        w_out.reshape(-1, LANES),
    )
    return pl.pallas_call(
        write_kernel,
        out_shape=(
            jax.ShapeDtypeStruct((rows, width), F32),
            jax.ShapeDtypeStruct((rows, width), F32),
            jax.ShapeDtypeStruct((width, hid), F32),
            jax.ShapeDtypeStruct((width, hid), F32),
            jax.ShapeDtypeStruct((tok, width), F32),
        ),
        in_specs=[vmem] * 5,
        out_specs=(hbm,) * 5,
        scratch_shapes=[
            pltpu.VMEM((rows, width), F32),
            pltpu.VMEM((rows, width), F32),
            pltpu.VMEM((width, hid), F32),
            pltpu.VMEM((width, hid), F32),
            dma((9,)),
        ],
        compiler_params=pltpu.CompilerParams(vmem_limit_bytes=16 * 1024 * 1024),
    )(total, table, accum, tower, emb_grad)


def solution(mesh):
    placed = (
        P(("dp", "emb")),
        P(("dp", "emb")),
        P(("dp", "emb"), None),
        P(),
        P("emb", None),
        P("emb", None),
        P("dp"),
        P(),
        P(None, "emb"),
        P(None, "emb"),
        P("emb"),
    )
    return jax.shard_map(
        on_device,
        mesh=mesh,
        in_specs=placed,
        out_specs=(
            P("emb", None),
            P("emb", None),
            P(None, "emb"),
            P(None, "emb"),
            P(("dp", "emb"), None),
        ),
        check_vma=False,
    )
```

time: 57.4 us -> 56.2 us (0.979)
  other arithmetic: 4.62 us -> 0 us
  local copies, waits for them, and re-layouts: 2.02 us -> 5.45 us
    unnamed x13 -> x22, local copies, waits for them, and re-layouts: 1.41 us -> 5.45 us
    sub x1 -> x0, other arithmetic: 2.48 us -> none  [on_device(): new_table = table - learn_rate * total * lax.rsqrt(new_accum)]
    convert_element_type x2 -> x0, other arithmetic: 2.14 us -> none  [on_device(): return (new_table, new_accum, gate.astype(F32), up.astype(F32), emb_grad)]
    pallas_call x0 -> x1, Pallas kernels: none -> 1.96 us  [on_device(): pl.pallas_call(write_kernel, out_shape=(jax.ShapeDtypeStruct((rows, width...]
    pallas_call x1, Pallas kernels: 49.6 us -> 47.7 us  [on_device(): pl.pallas_call(functools.partial(tower_kernel, n_dp, n_emb, scale), out_s...]
    reshape x1 -> x0, local copies, waits for them, and re-layouts: 0.6 us -> none  [on_device(): w_out.reshape(1, -1)]
where the time goes in v1:
time: 56.2 us; the launch traced here: 55.8 us
  Pallas kernels  49.6 us (88%)
  local copies, waits for them, and re-layouts  5.45 us (10%)
  between operations  0.7 us (1%)
    pallas_call x1, Pallas kernels, on_device(): pl.pallas_call(functools.partial(tower_kernel, n_dp, n_emb, scale), out_s...  47.7 us
    unnamed x22, local copies, waits for them, and re-layouts  5.45 us
    pallas_call x1, Pallas kernels, on_device(): pl.pallas_call(write_kernel, out_shape=(jax.ShapeDtypeStruct((rows, width...  1.96 us

profile of v1, /device:TPU:0, one launch (start us, length us, event | category | flops | bytes accessed | tf_op | source)
XLA Modules:
  0.0 55.8 jit_solution(10019919071450640870)
XLA Ops:
  0.6 0.0 copy-start.9
  0.6 0.0 copy-start.6
  0.7 0.0 copy-start.7
  0.7 0.0 copy-start.8
  0.7 0.0 copy-start.10
  0.7 0.6 %copy-done.9 = s32[256]{0:T(256)S(1)} copy-done((s32[256]{0:T(256)S(1)}, s32[256]{0:T(256)}, u32[]{:S(2)}) %copy-start.9) | copy-done | bytes 1048
  1.3 0.0 copy-done.6
  1.3 0.0 copy-done.7
  1.4 0.0 copy-done.8
  1.4 0.0 copy-done.10
  1.4 0.0 copy-start
  1.4 1.1 %copy-done = f32[1536,128]{1,0:T(8,128)S(1)} copy-done((f32[1536,128]{1,0:T(8,128)S(1)}, f32[1536,128]{1,0:T(8,128)}, u32[]{:S(2)}) %copy-start) | copy-done | bytes 786456
  2.5 0.0 copy-start.2
  2.5 1.0 %copy-done.2 = bf16[128,2048]{1,0:T(8,128)(2,1)S(1)} copy-done((bf16[128,2048]{1,0:T(8,128)(2,1)S(1)}, bf16[128,2048]{1,0:T(8,128)(2,1)}, u32[]{:S(2)}) %copy-start.2) | copy-done | bytes 524312
  3.5 0.0 copy-start.3
  3.5 1.0 %copy-done.3 = bf16[128,2048]{1,0:T(8,128)(2,1)S(1)} copy-done((bf16[128,2048]{1,0:T(8,128)(2,1)S(1)}, bf16[128,2048]{1,0:T(8,128)(2,1)}, u32[]{:S(2)}) %copy-start.3) | copy-done | bytes 524312
  4.6 0.0 copy-start.4
  4.6 0.8 %copy-done.4 = bf16[256,128]{1,0:T(8,128)(2,1)S(1)} copy-done((bf16[256,128]{1,0:T(8,128)(2,1)S(1)}, bf16[256,128]{1,0:T(8,128)(2,1)}, u32[]{:S(2)}) %copy-start.4) | copy-done | bytes 65560
  5.4 0.0 copy-start.5
  5.4 0.7 %copy-done.5 = s32[3072]{0:T(1024)S(1)} copy-done((s32[3072]{0:T(1024)S(1)}, s32[3072]{0:T(1024)}, u32[]{:S(2)}) %copy-start.5) | copy-done | bytes 12312
  6.1 0.0 copy-start.1
  6.1 47.7 %shard_map.146 = (bf16[1536,128]{1,0:T(8,128)(2,1)S(1)}, bf16[4096,128]{1,0:T(8,128)(2,1)S(1)}, f32[256,128]{1,0:T(8,128)S(1)}) custom-call(s32[1,256]{1,0:T(1,128)S(1)} %bitcast.9, s32[1,256]{1,0:T(1,128)S(1)} %bitcast.10, bf16[256,128]{1,0:T(8,128)(2,1)S(1)} %copy-done.4, s32[24,128]{1,0:T(8,128)S(1)} %bitcast.6, f32[1536,128]{1,0:T(8,128)S(1)} %copy-done, ...), custom_call_target="tpu_custom_call" | custom-call | tf_op jit(solution)/shard_map/pallas_call | solution.py:558
  53.8 0.0 copy-done.1
  53.8 2.0 %shard_map.147 = (f32[1536,128]{1,0:T(8,128)}, f32[1536,128]{1,0:T(8,128)}, f32[128,2048]{1,0:T(8,128)}, f32[128,2048]{1,0:T(8,128)}, f32[256,128]{1,0:T(8,128)}) custom-call(bf16[1536,128]{1,0:T(8,128)(2,1)S(1)} %get-tuple-element.8.total_ref, f32[1536,128]{1,0:T(8,128)S(1)} %copy-done, f32[1536,128]{1,0:T(8,128)S(1)} %copy-done.1, ...), custom_call_target="tpu_custom_call" | custom-call | tf_op jit(solution)/shard_map/pallas_call | solution.py:620
Async XLA Ops:
  0.6 0.7 %copy-start.9 = (s32[256]{0:T(256)S(1)}, s32[256]{0:T(256)}, u32[]{:S(2)}) copy-start(s32[256]{0:T(256)} %param.12) | copy-start | bytes 3076
  0.6 0.7 %copy-start.6 = (bf16[2048]{0:T(1024)(128)(2,1)S(1)}, bf16[2048]{0:T(1024)(128)(2,1)}, u32[]{:S(2)}) copy-start(bf16[2048]{0:T(1024)(128)(2,1)} %param.21) | copy-start | bytes 12292
  0.7 0.7 %copy-start.7 = (f32[512]{0:T(512)S(1)}, f32[512]{0:T(512)}, u32[]{:S(2)}) copy-start(f32[512]{0:T(512)} %param.17) | copy-start | bytes 6148
  0.7 0.7 %copy-start.8 = (s32[256]{0:T(256)S(1)}, s32[256]{0:T(256)}, u32[]{:S(2)}) copy-start(s32[256]{0:T(256)} %param.11) | copy-start | bytes 3076
  0.7 0.7 %copy-start.10 = (f32[128]{0:T(128)S(1)}, f32[128]{0:T(128)}, u32[]{:S(2)}) copy-start(f32[128]{0:T(128)} %param.18) | copy-start | bytes 1540
  1.4 1.1 %copy-start = (f32[1536,128]{1,0:T(8,128)S(1)}, f32[1536,128]{1,0:T(8,128)}, u32[]{:S(2)}) copy-start(f32[1536,128]{1,0:T(8,128)} %table_ref.3) | copy-start | bytes 2359300
  2.5 1.0 %copy-start.2 = (bf16[128,2048]{1,0:T(8,128)(2,1)S(1)}, bf16[128,2048]{1,0:T(8,128)(2,1)}, u32[]{:S(2)}) copy-start(bf16[128,2048]{1,0:T(8,128)(2,1)} %wg_ref.1) | copy-start | bytes 1572868
  3.5 1.0 %copy-start.3 = (bf16[128,2048]{1,0:T(8,128)(2,1)S(1)}, bf16[128,2048]{1,0:T(8,128)(2,1)}, u32[]{:S(2)}) copy-start(bf16[128,2048]{1,0:T(8,128)(2,1)} %wu_ref.1) | copy-start | bytes 1572868
  4.6 0.8 %copy-start.4 = (bf16[256,128]{1,0:T(8,128)(2,1)S(1)}, bf16[256,128]{1,0:T(8,128)(2,1)}, u32[]{:S(2)}) copy-start(bf16[256,128]{1,0:T(8,128)(2,1)} %grads_ref.1) | copy-start | bytes 196612
  5.4 0.7 %copy-start.5 = (s32[3072]{0:T(1024)S(1)}, s32[3072]{0:T(1024)}, u32[]{:S(2)}) copy-start(s32[3072]{0:T(1024)} %param.14) | copy-start | bytes 36868
  6.1 47.7 %copy-start.1 = (f32[1536,128]{1,0:T(8,128)S(1)}, f32[1536,128]{1,0:T(8,128)}, u32[]{:S(2)}) copy-start(f32[1536,128]{1,0:T(8,128)} %accum_ref.1) | copy-start | bytes 2359300

commit v2 on v1

--- a/solution.py
+++ b/solution.py
@@ -26,24 +26,32 @@
 
 
 class Reduce:
-    def __init__(self, at, copy, pending, bufs, send, recv):
-        self.at, self.copy, self.pending = at, copy, pending
+    def __init__(self, at, copy, bufs, send, recv):
+        self.at, self.copy = at, copy
         self.part, self.pair, self.x_out, self.keep, self.x_in, self.z_out, self.z_in, self.full = bufs
         self.send, self.recv = send, recv
         self.half = self.pair.shape[0]
         self.quarter = self.half // 2
-        self.size = self.quarter // at["n_hi"]
+        n_hi = at["n_hi"]
+        self.size = self.quarter // n_hi
+        self.subs = subs_of(self.size)
+        self.bits = [1 << b for b in reversed(range(n_hi.bit_length() - 1))]
+        self.masks = sorted(range(1, n_hi), key=lambda m: (-(m & -m), m))
+        self.base = recv_layout(n_hi, self.subs)[0]
 
     def rows(self, start, size):
         return pl.ds(pl.multiple_of(start, math.gcd(size, 128)), size)
 
-    def place(self, lo, hi):
-        return self.rows(self.at["par"] * self.half + lo * self.quarter + hi * self.size, self.size)
+    def place(self, lo, hi, sub=None):
+        start = self.at["par"] * self.half + lo * self.quarter + hi * self.size
+        if sub is None:
+            return self.rows(start, self.size)
+        step = self.size // self.subs
+        return self.rows(start + sub * step, step)
 
     def go(self, src, dst, stage, k, dp):
-        one = self.copy(src, dst, self.send.at[stage, k], self.recv.at[stage, k], dp, self.at["emb"])
+        one = self.copy(src, dst, self.send.at[stage], self.recv.at[self.base[stage] + k], dp, self.at["emb"])
         one.start()
-        self.pending.append(one)
         return one
 
     def start(self, away):
@@ -86,7 +94,7 @@
         for k in range(1, self.at["n_hi"]):
             self.z_out[k - 1] = self.joined(k).astype(BF16)
             self.z.append(
-                self.go(self.z_out.at[k - 1], self.z_in.at[k - 1], 2, k, self.at["far"][k])
+                self.go(self.z_out.at[k - 1], self.z_in.at[k - 1], 2, k - 1, self.at["far"][k])
             )
 
     def stage_sum(self):
@@ -95,32 +103,82 @@
         for k, one in enumerate(self.z):
             one.wait_recv()
             total = total + self.z_in[k].astype(F32)
-        mine = self.place(at["low"], at["high"])
-        self.full[mine, :] = total.astype(BF16)
-        view = self.full.at[mine]
-        self.spread = [self.go(view, view, 3, k, at["far"][k]) for k in range(1, at["n_hi"])]
-        self.near = [self.go(view, view, 4, 0, at["beside"])]
-        self.last = [self.go(view, view, 5, 0, at["partner"])]
-
-    def spread_z(self):
+        self.full[self.place(at["low"], at["high"]), :] = total.astype(BF16)
+        self.far, self.near = {}, {}
+        for bit in self.bits:
+            for sub in range(self.subs):
+                self.pass_on(0, sub, bit)
+        for sub in range(self.subs):
+            self.pass_near(0, sub)
+
+    def pass_on(self, mask, sub, bit):
         at = self.at
-        for k in range(1, at["n_hi"]):
-            self.spread[k - 1].wait_recv()
-            view = self.full.at[self.place(at["low"], at["behind"][k])]
-            self.near.append(self.go(view, view, 4, k, at["beside"]))
-            self.last.append(self.go(view, view, 5, k, at["partner"]))
-
-    def spread_x(self):
+        view = self.full.at[self.place(at["low"], flip(at["high"], mask), sub)]
+        got = mask | bit
+        peer = (2 * flip(at["high"], bit) + at["low"]) * 2 + at["par"]
+        self.far[got, sub] = self.go(view, view, 3, self.masks.index(got) * self.subs + sub, peer)
+
+    def pass_near(self, mask, sub):
         at = self.at
-        n_hi = at["n_hi"]
-        for k in range(n_hi):
-            self.near[k].wait_recv()
-            view = self.full.at[self.place(1 - at["low"], at["behind"][k])]
-            self.last.append(self.go(view, view, 5, n_hi + k, at["partner"]))
+        view = self.full.at[self.place(at["low"], flip(at["high"], mask), sub)]
+        self.near[mask, sub] = self.go(view, view, 4, mask * self.subs + sub, at["beside"])
+        self.go(view, view, 5, 0, at["partner"])
+
+    def take_far(self, mask, sub):
+        self.far[mask, sub].wait_recv()
+        for bit in self.bits:
+            if bit < (mask & -mask):
+                self.pass_on(mask, sub, bit)
+        self.pass_near(mask, sub)
+
+    def take_near(self, mask, sub):
+        self.near[mask, sub].wait_recv()
+        view = self.full.at[self.place(1 - self.at["low"], flip(self.at["high"], mask), sub)]
+        self.go(view, view, 5, 0, self.at["partner"])
+
+    def spread(self):
+        far = [(mask, sub) for mask in self.masks for sub in range(self.subs)]
+        near = [(0, sub) for sub in range(self.subs)] + far
+        for i, item in enumerate(far):
+            self.take_far(*item)
+            if i >= self.subs:
+                self.take_near(*near[i - self.subs])
+        for item in near[len(far) - self.subs :]:
+            self.take_near(*item)
 
     def finish(self):
-        for one in self.last:
-            one.wait_recv()
+        partner = self.at["partner"]
+
+        def sizes(ref, stage, k=0):
+            return self.copy(ref, ref, self.send.at[stage], self.recv.at[self.base[stage] + k], partner, self.at["emb"])
+
+        whole = self.full.at[self.rows((1 - self.at["par"]) * self.half, self.half)]
+        sizes(whole, 5).wait_recv()
+        sizes(self.pair, 0).wait_send()
+        sizes(self.x_out, 1).wait_send()
+        sizes(self.z_out, 2).wait_send()
+        sizes(self.z_out, 3).wait_send()
+        sizes(self.x_out, 4).wait_send()
+        sizes(whole, 5).wait_send()
+
+
+def flip(index, mask):
+    bit = 1
+    while bit <= mask:
+        if mask & bit:
+            index = index + bit * (1 - 2 * ((index // bit) % 2))
+        bit *= 2
+    return index
+
+
+def subs_of(size):
+    return 2 if size % 256 == 0 else 1
+
+
+def recv_layout(n_hi, subs):
+    counts = [2, n_hi, n_hi - 1, (n_hi - 1) * subs, n_hi * subs, 1]
+    starts = [sum(counts[:i]) for i in range(len(counts))]
+    return starts, sum(counts)
 
 
 def tower_kernel(
@@ -155,7 +213,6 @@
     contrib,
     lbuf,
     values,
-    normed,
     normed_t,
     act,
     logit_acc,
@@ -230,10 +287,10 @@
     )
     pending = []
     sums = Reduce(
-        at, copy, pending, (tpart, tpair, tx_out, tkeep, tx_in, tz_out, tz_in, tall), t_send, t_recv
+        at, copy, (tpart, tpair, tx_out, tkeep, tx_in, tz_out, tz_in, tall), t_send, t_recv
     )
     tower = Reduce(
-        at, copy, pending, (gpart, gpair, gx_out, gkeep, gx_in, gz_out, gz_in, gall_sum), g_send, g_recv
+        at, copy, (gpart, gpair, gx_out, gkeep, gx_in, gz_out, gz_in, gall_sum), g_send, g_recv
     )
 
     barrier = pltpu.get_barrier_semaphore()
@@ -264,22 +321,21 @@
     loads[1].wait()
     pl.semaphore_wait(barrier, n_emb - 1 + n_hi - 1 + 2)
 
-    def to_peers(src, dst_of, stage, slot, peers=None):
+    def to_peers(src, dst_of, peers=None):
         sent = []
         for k in peers or range(1, n_emb):
-            one = copy(
-                src(k), dst_of(k), e_send.at[stage, slot, k - 1], e_recv.at[stage, slot, k - 1], me_dp, other_emb(k)
-            )
+            slot = len(pending)
+            one = copy(src, dst_of(k), e_send.at[slot], e_recv.at[slot], me_dp, other_emb(k))
             one.start()
             sent.append(one)
-        pending.extend(sent)
+            pending.append(one)
         return sent
 
     own_ids = ids.at[me_emb]
-    id_copies = to_peers(lambda k: own_ids, lambda k: own_ids, 0, 0)
+    id_copies = to_peers(own_ids, lambda k: own_ids)
     loads[3].wait()
     own_grads = gall.at[me_emb]
-    grad_copies = to_peers(lambda k: own_grads, lambda k: own_grads, 1, 0)
+    grad_copies = to_peers(own_grads, lambda k: own_grads)
 
     loads[2].wait()
     groups = place.shape[0]
@@ -316,10 +372,8 @@
             acc = acc + dot(hot, table16[i * kt : (i + 1) * kt, :])
         view = contrib.at[tokens(e)]
         contrib[tokens(e), :] = acc.astype(BF16)
-        for k, one in zip(
-            range(1, n_emb), to_peers(lambda k: view, lambda k: lbuf.at[k - 1, tokens(e)], 2, s)
-        ):
-            row_copies[k, s] = one
+        for k, one in enumerate(to_peers(view, lambda k: lbuf.at[k - 1, tokens(e)])):
+            row_copies[k + 1, s] = one
         prev_pos.append((e, place_of(ids[e, 1]) - base))
 
     for one in grad_copies:
@@ -328,7 +382,7 @@
     pt = 128 if half_rows % 128 == 0 else half_rows
 
     def grad_half(which):
-        def grad_step(i, carry):
+        for i in range(half_rows // pt):
             at_row = pl.multiple_of(which * half_rows + i * pt, pt)
             index = lax.broadcasted_iota(jnp.int32, (pt, tok), 0) + at_row
             acc = jnp.zeros((pt, LANES), F32)
@@ -336,9 +390,6 @@
                 hot = jnp.where(index == pos, 1.0, 0.0).astype(BF16)
                 acc = acc + dot(hot, gall[e])
             tpart[pl.ds(at_row, pt), :] = acc
-            return carry
-
-        lax.fori_loop(0, half_rows // pt, grad_step, 0)
 
     grad_half(1 - par)
     sums.start(True)
@@ -353,18 +404,6 @@
         parts = [wo_row[pl.ds(j * per_tile + b, 1), :] for b in range(per_tile)]
         return jnp.concatenate(parts, axis=1)
 
-    sums.stage_x()
-
-    def scale_step(j, carry):
-        cols = pl.ds(pl.multiple_of(j * ht, ht), ht)
-        head = head_of(j)
-        scaled_w[0, :, cols] = (wg[:, cols].astype(F32) * head).astype(BF16)
-        scaled_w[1, :, cols] = (wu[:, cols].astype(F32) * head).astype(BF16)
-        return carry
-
-    lax.fori_loop(0, tiles, scale_step, 0)
-    sums.stage_keep()
-
     def forward(e):
         span = tokens(e)
         looked = contrib[span, :].astype(F32)
@@ -373,38 +412,25 @@
         values[span, :] = looked
         inverse_rms = lax.rsqrt(jnp.mean(looked * looked, axis=1, keepdims=True) + norm_eps)
         norm = (looked * inverse_rms * gain[...]).astype(BF16)
-        normed[span, :] = norm
+        norm_half = norm * jnp.asarray(0.5, BF16)
         normed_t[:, span] = norm.astype(F32).T
-        logit_acc[...] = jnp.zeros_like(logit_acc)
-
-        def tower_step(j, carry):
-            cols = pl.ds(pl.multiple_of(j * ht, ht), ht)
-            gate = dot(normed[span, :], wg[:, cols])
-            up = dot(normed[span, :], wu[:, cols])
-            sig = 0.5 + 0.5 * jnp.tanh(0.5 * gate)
-            activated = gate * sig
-            act[0, span, cols] = (up * (sig + activated * (1.0 - sig))).astype(BF16)
-            act[1, span, cols] = activated.astype(BF16)
-            weighed = activated * up * head_of(j)
+        logit_sum = jnp.zeros((tok, LANES), F32)
+        logit_acc[...] = logit_sum
+        for j in range(tiles):
+            cols = slice(j * ht, (j + 1) * ht)
+            half_gate = dot(norm_half, wg[:, cols])
+            up = dot(norm, wu[:, cols])
+            t = jnp.tanh(half_gate)
+            above = 1.0 + t
+            risen = up * above
+            act[0, span, cols] = (risen * (1.0 + half_gate * (1.0 - t))).astype(BF16)
+            act[1, span, cols] = (half_gate * above).astype(BF16)
+            weighed = half_gate * risen * head_of(j)
             part = weighed[:, 0:LANES]
             for b in range(1, per_tile):
                 part = part + weighed[:, b * LANES : (b + 1) * LANES]
             logit_acc[...] += part
-            return carry
-
-        lax.fori_loop(0, tiles, tower_step, 0)
         logit[e] = jnp.sum(logit_acc[...].T, axis=0, keepdims=True)
-
-    def backward(e):
-        span = tokens(e)
-
-        def back_step(j, carry):
-            cols = pl.ds(pl.multiple_of(j * ht, ht), ht)
-            return carry + dot_nt(act[0, span, cols], scaled_w[0, :, cols]) + dot_nt(
-                act[1, span, cols], scaled_w[1, :, cols]
-            )
-
-        bn[span, :] = lax.fori_loop(0, tiles, back_step, jnp.zeros((tok, LANES), F32))
 
     logit_copies = []
     for q in range(1, n_emb + 1):
@@ -413,18 +439,11 @@
             row_copies[k, (k - q) % n_emb].wait_recv()
         forward(e)
         view = logit.at[e]
-        logit_copies += to_peers(lambda k: view, lambda k: logit_in.at[k - 1, e], 3, q - 1)
+        logit_copies += to_peers(view, lambda k: logit_in.at[k - 1, e])
         if q == 1:
-            sums.stage_z()
-    back_copies = []
-    for q in range(1, n_emb):
-        e = other_emb(n_emb - q)
-        backward(e)
-        k = n_emb - q
-        view = bn.at[tokens(e)]
-        back_copies += to_peers(lambda k: view, lambda k: bn_in.at[k - 1], 4, 0, [k])
-    backward(me_emb)
-    sums.stage_sum()
+            sums.stage_x()
+    sums.stage_keep()
+    sums.stage_z()
 
     for one in logit_copies:
         one.wait_recv()
@@ -438,26 +457,41 @@
         lead[:, span] = (normed_t[:, span] * slope).astype(BF16)
 
     def weight_grads(which, lo):
-        def step(i, carry):
+        factor = scale * (0.5 + 0.5 * which.astype(F32))
+        for i in range(tiles // 2):
             j = lo * (tiles // 2) + i
             cols = pl.ds(pl.multiple_of(j * ht, ht), ht)
-            part = (dot(lead[...], act[which, :, cols]) * (head_of(j) * scale)).astype(BF16)
+            part = (dot(lead[...], act[which, :, cols]) * (head_of(j) * factor)).astype(BF16)
             for b in range(per_tile):
                 to = which * hid + j * ht + b * LANES
                 gpart[pl.ds(pl.multiple_of(to, LANES), LANES), :] = part[:, b * LANES : (b + 1) * LANES]
-            return carry
-
-        lax.fori_loop(0, tiles // 2, step, 0)
 
     weight_grads(1 - par, 1 - low)
     tower.start(True)
     weight_grads(par, 1 - low)
+    tower.stage_x()
     weight_grads(1 - par, low)
     tower.start(False)
-    tower.stage_x()
     weight_grads(par, low)
     tower.stage_keep()
-    sums.spread_z()
+    sums.stage_sum()
+
+    for j in range(tiles):
+        cols = slice(j * ht, (j + 1) * ht)
+        head = head_of(j)
+        scaled_w[0, :, cols] = (wg[:, cols].astype(F32) * (0.5 * head)).astype(BF16)
+        scaled_w[1, :, cols] = (wu[:, cols].astype(F32) * head).astype(BF16)
+    back_copies = []
+    for q in range(1, n_emb + 1):
+        e = other_emb(n_emb - q)
+        span = tokens(e)
+        bn[span, :] = dot_nt(act[0, span, :], scaled_w[0]) + dot_nt(act[1, span, :], scaled_w[1])
+        if q < n_emb:
+            back_copies += to_peers(bn.at[span], lambda k: bn_in.at[k - 1], [n_emb - q])
+
+    tower.stage_z()
+    sums.spread()
+    tower.stage_sum()
 
     for one in back_copies:
         one.wait_recv()
@@ -473,13 +507,9 @@
         x * scaled, axis=1, keepdims=True
     )
 
-    tower.stage_z()
-    sums.spread_x()
-    tower.stage_sum()
+    tower.spread()
     sums.finish()
     total_ref[...] = tall[...]
-    tower.spread_z()
-    tower.spread_x()
     tower.finish()
     tower_ref[...] = gall_sum[...]
     for one in pending:
@@ -540,6 +570,7 @@
     n_peer = max(n_emb - 1, 1)
     dma = pltpu.SemaphoreType.DMA
     I32 = jnp.int32
+    emb_copies = max((n_emb - 1) * (2 * n_emb + 3), 1)
 
     def reduce_buffers(total_rows, dtype):
         half = total_rows // 2
@@ -580,7 +611,6 @@
             pltpu.VMEM((group, width), BF16),
             pltpu.VMEM((n_peer, group, width), BF16),
             pltpu.VMEM((group, width), F32),
-            pltpu.VMEM((group, width), BF16),
             pltpu.VMEM((width, group), F32),
             pltpu.VMEM((2, group, hid), BF16),
             pltpu.VMEM((tok, width), F32),
@@ -595,27 +625,32 @@
         + reduce_buffers(2 * hid, BF16)
         + [
             dma((10,)),
-            dma((5, n_emb, n_peer)),
-            dma((5, n_emb, n_peer)),
-            dma((6, 2 * n_hi)),
-            dma((6, 2 * n_hi)),
-            dma((6, 2 * n_hi)),
-            dma((6, 2 * n_hi)),
+            dma((emb_copies,)),
+            dma((emb_copies,)),
+            dma((6,)),
+            dma((recv_layout(n_hi, subs_of(rows // 4 // n_hi))[1],)),
+            dma((6,)),
+            dma((recv_layout(n_hi, subs_of(hid // 2 // n_hi))[1],)),
         ],
         compiler_params=pltpu.CompilerParams(
             collective_id=0, has_side_effects=True, vmem_limit_bytes=40 * 1024 * 1024
         ),
     )(
-        cur_ids.reshape(1, -1),
-        prev_ids.reshape(1, -1),
-        prev_grads,
-        row_place.reshape(-1, LANES),
-        table,
-        labels.reshape(n_emb, 1, -1),
-        gain.reshape(1, -1),
-        w_gate,
-        w_up,
-        w_out.reshape(-1, LANES),
+        *[
+            pltpu.with_memory_space_constraint(x, pltpu.HBM)
+            for x in (
+                cur_ids.reshape(1, -1),
+                prev_ids.reshape(1, -1),
+                prev_grads,
+                row_place.reshape(-1, LANES),
+                table,
+                labels.reshape(n_emb, 1, -1),
+                gain.reshape(1, -1),
+                w_gate,
+                w_up,
+                w_out.reshape(-1, LANES),
+            )
+        ]
     )
     return pl.pallas_call(
         write_kernel,

time: 56.2 us -> 45.1 us (0.80)
  local copies, waits for them, and re-layouts: 5.45 us -> 0.01 us
  Pallas kernels: 49.6 us -> 44.2 us
    unnamed x22 -> x4, local copies, waits for them, and re-layouts: 5.45 us -> 0.01 us
    pallas_call x1, Pallas kernels: 47.7 us -> 42.3 us  [on_device(): pl.pallas_call(functools.partial(tower_kernel, n_dp, n_emb, scale), out_s...]
where the time goes in v2:
time: 45.1 us; the launch traced here: 44.9 us
  Pallas kernels  44.2 us (98%)
  between operations  0.68 us (2%)
    pallas_call x1, Pallas kernels, on_device(): pl.pallas_call(functools.partial(tower_kernel, n_dp, n_emb, scale), out_s...  42.3 us
    pallas_call x1, Pallas kernels, on_device(): pl.pallas_call(write_kernel, out_shape=(jax.ShapeDtypeStruct((rows, width...  1.96 us

profile of v2, /device:TPU:0, one launch (start us, length us, event | category | flops | bytes accessed | tf_op | source)
XLA Modules:
  0.0 44.9 jit_solution(16277778648933810539)
XLA Ops:
  0.6 0.0 copy-start
  0.6 0.0 copy-start.1
  0.7 42.3 %shard_map.146 = (bf16[1536,128]{1,0:T(8,128)(2,1)S(1)}, bf16[4096,128]{1,0:T(8,128)(2,1)S(1)}, f32[256,128]{1,0:T(8,128)S(1)}) custom-call(s32[1,256]{1,0:T(1,128)} %bitcast.9, s32[1,256]{1,0:T(1,128)} %bitcast.10, bf16[256,128]{1,0:T(8,128)(2,1)} %grads_ref.1, s32[24,128]{1,0:T(8,128)} %bitcast.6, f32[1536,128]{1,0:T(8,128)} %table_ref.3, ...), custom_call_target="tpu_custom_call" | custom-call | tf_op jit(solution)/shard_map/pallas_call | solution.py:589
  42.9 0.0 copy-done
  42.9 0.0 copy-done.1
  43.0 2.0 %shard_map.147 = (f32[1536,128]{1,0:T(8,128)}, f32[1536,128]{1,0:T(8,128)}, f32[128,2048]{1,0:T(8,128)}, f32[128,2048]{1,0:T(8,128)}, f32[256,128]{1,0:T(8,128)}) custom-call(bf16[1536,128]{1,0:T(8,128)(2,1)S(1)} %get-tuple-element.8.total_ref, f32[1536,128]{1,0:T(8,128)S(1)} %copy-done, f32[1536,128]{1,0:T(8,128)S(1)} %copy-done.1, ...), custom_call_target="tpu_custom_call" | custom-call | tf_op jit(solution)/shard_map/pallas_call | solution.py:655
Async XLA Ops:
  0.6 42.3 %copy-start = (f32[1536,128]{1,0:T(8,128)S(1)}, f32[1536,128]{1,0:T(8,128)}, u32[]{:S(2)}) copy-start(f32[1536,128]{1,0:T(8,128)} %table_ref.3) | copy-start | bytes 2359300
  0.6 42.3 %copy-start.1 = (f32[1536,128]{1,0:T(8,128)S(1)}, f32[1536,128]{1,0:T(8,128)}, u32[]{:S(2)}) copy-start(f32[1536,128]{1,0:T(8,128)} %accum_ref.1) | copy-start | bytes 2359300

commit v3 on v2

--- a/solution.py
+++ b/solution.py
@@ -67,7 +67,7 @@
     def stage_x(self):
         at = self.at
         self.first_away.wait_recv()
-        self.x = {}
+        self.x, self.z = {}, {}
         lo = (1 - at["low"]) * self.quarter
         for k in list(range(1, at["n_hi"])) + [0]:
             piece = at["ahead"][k] * self.size
@@ -89,20 +89,18 @@
         kept = self.keep[self.rows(self.at["ahead"][k] * self.size, self.size), :]
         return kept + self.x_in[k].astype(F32)
 
-    def stage_z(self):
-        self.z = []
-        for k in range(1, self.at["n_hi"]):
-            self.z_out[k - 1] = self.joined(k).astype(BF16)
-            self.z.append(
-                self.go(self.z_out.at[k - 1], self.z_in.at[k - 1], 2, k - 1, self.at["far"][k])
-            )
+    def stage_z(self, k):
+        self.z_out[k - 1] = self.joined(k).astype(BF16)
+        self.z[k] = self.go(
+            self.z_out.at[k - 1], self.z_in.at[k - 1], 2, k - 1, self.at["far"][k]
+        )
 
     def stage_sum(self):
         at = self.at
         total = self.joined(0)
-        for k, one in enumerate(self.z):
-            one.wait_recv()
-            total = total + self.z_in[k].astype(F32)
+        for k in range(1, at["n_hi"]):
+            self.z[k].wait_recv()
+            total = total + self.z_in[k - 1].astype(F32)
         self.full[self.place(at["low"], at["high"]), :] = total.astype(BF16)
         self.far, self.near = {}, {}
         for bit in self.bits:
@@ -172,7 +170,7 @@
 
 
 def subs_of(size):
-    return 2 if size % 256 == 0 else 1
+    return 4 if size % 256 == 0 else 1
 
 
 def recv_layout(n_hi, subs):
@@ -333,10 +331,6 @@
 
     own_ids = ids.at[me_emb]
     id_copies = to_peers(own_ids, lambda k: own_ids)
-    loads[3].wait()
-    own_grads = gall.at[me_emb]
-    grad_copies = to_peers(own_grads, lambda k: own_grads)
-
     loads[2].wait()
     groups = place.shape[0]
     stored = place[...]
@@ -374,10 +368,12 @@
         contrib[tokens(e), :] = acc.astype(BF16)
         for k, one in enumerate(to_peers(view, lambda k: lbuf.at[k - 1, tokens(e)])):
             row_copies[k + 1, s] = one
+        if s == 0:
+            loads[3].wait()
+            own_grads = gall.at[me_emb]
+            grad_copies = to_peers(own_grads, lambda k: own_grads)
         prev_pos.append((e, place_of(ids[e, 1]) - base))
 
-    for one in grad_copies:
-        one.wait_recv()
     half_rows = rows // 2
     pt = 128 if half_rows % 128 == 0 else half_rows
 
@@ -391,10 +387,6 @@
                 acc = acc + dot(hot, gall[e])
             tpart[pl.ds(at_row, pt), :] = acc
 
-    grad_half(1 - par)
-    sums.start(True)
-    sums.start(False)
-    grad_half(par)
     for one in loads[5:]:
         one.wait()
     wo_row[...] = wo[...].astype(F32)
@@ -441,9 +433,14 @@
         view = logit.at[e]
         logit_copies += to_peers(view, lambda k: logit_in.at[k - 1, e])
         if q == 1:
-            sums.stage_x()
+            for one in grad_copies:
+                one.wait_recv()
+            grad_half(1 - par)
+            sums.start(True)
+            sums.start(False)
+            grad_half(par)
+    sums.stage_x()
     sums.stage_keep()
-    sums.stage_z()
 
     for one in logit_copies:
         one.wait_recv()
@@ -470,11 +467,16 @@
     tower.start(True)
     weight_grads(par, 1 - low)
     tower.stage_x()
+    for k in range(1, n_hi):
+        sums.stage_z(k)
     weight_grads(1 - par, low)
     tower.start(False)
     weight_grads(par, low)
     tower.stage_keep()
+    tower.stage_z(1)
     sums.stage_sum()
+    for k in range(2, n_hi):
+        tower.stage_z(k)
 
     for j in range(tiles):
         cols = slice(j * ht, (j + 1) * ht)
@@ -489,9 +491,12 @@
         if q < n_emb:
             back_copies += to_peers(bn.at[span], lambda k: bn_in.at[k - 1], [n_emb - q])
 
-    tower.stage_z()
-    sums.spread()
+    for mask in sums.masks:
+        sums.take_far(mask, 0)
     tower.stage_sum()
+    sums.take_near(0, 0)
+    for mask in sums.masks:
+        sums.take_near(mask, 0)
 
     for one in back_copies:
         one.wait_recv()

time: 45.1 us -> 43.4 us (0.962)
  Pallas kernels: 44.2 us -> 42.5 us
    pallas_call x1, Pallas kernels: 42.3 us -> 40.6 us  [on_device(): pl.pallas_call(functools.partial(tower_kernel, n_dp, n_emb, scale), out_s...]
where the time goes in v3:
time: 43.4 us; the launch traced here: 43.2 us
  Pallas kernels  42.5 us (98%)
  between operations  0.68 us (2%)
    pallas_call x1, Pallas kernels, on_device(): pl.pallas_call(functools.partial(tower_kernel, n_dp, n_emb, scale), out_s...  40.6 us
    pallas_call x1, Pallas kernels, on_device(): pl.pallas_call(write_kernel, out_shape=(jax.ShapeDtypeStruct((rows, width...  1.96 us

profile of v3, /device:TPU:0, one launch (start us, length us, event | category | flops | bytes accessed | tf_op | source)
XLA Modules:
  0.0 43.2 jit_solution(5710631774557347002)
XLA Ops:
  0.6 0.0 copy-start
  0.6 0.0 copy-start.1
  0.7 40.6 %shard_map.146 = (bf16[1536,128]{1,0:T(8,128)(2,1)S(1)}, bf16[4096,128]{1,0:T(8,128)(2,1)S(1)}, f32[256,128]{1,0:T(8,128)S(1)}) custom-call(s32[1,256]{1,0:T(1,128)} %bitcast.9, s32[1,256]{1,0:T(1,128)} %bitcast.10, bf16[256,128]{1,0:T(8,128)(2,1)} %grads_ref.1, s32[24,128]{1,0:T(8,128)} %bitcast.6, f32[1536,128]{1,0:T(8,128)} %table_ref.3, ...), custom_call_target="tpu_custom_call" | custom-call | tf_op jit(solution)/shard_map/pallas_call | solution.py:594
  41.2 0.0 copy-done
  41.3 0.0 copy-done.1
  41.3 2.0 %shard_map.147 = (f32[1536,128]{1,0:T(8,128)}, f32[1536,128]{1,0:T(8,128)}, f32[128,2048]{1,0:T(8,128)}, f32[128,2048]{1,0:T(8,128)}, f32[256,128]{1,0:T(8,128)}) custom-call(bf16[1536,128]{1,0:T(8,128)(2,1)S(1)} %get-tuple-element.8.total_ref, f32[1536,128]{1,0:T(8,128)S(1)} %copy-done, f32[1536,128]{1,0:T(8,128)S(1)} %copy-done.1, ...), custom_call_target="tpu_custom_call" | custom-call | tf_op jit(solution)/shard_map/pallas_call | solution.py:660
Async XLA Ops:
  0.6 40.6 %copy-start = (f32[1536,128]{1,0:T(8,128)S(1)}, f32[1536,128]{1,0:T(8,128)}, u32[]{:S(2)}) copy-start(f32[1536,128]{1,0:T(8,128)} %table_ref.3) | copy-start | bytes 2359300
  0.6 40.6 %copy-start.1 = (f32[1536,128]{1,0:T(8,128)S(1)}, f32[1536,128]{1,0:T(8,128)}, u32[]{:S(2)}) copy-start(f32[1536,128]{1,0:T(8,128)} %accum_ref.1) | copy-start | bytes 2359300

commit v4 on v3

--- a/solution.py
+++ b/solution.py
@@ -30,79 +30,76 @@
         self.at, self.copy = at, copy
         self.part, self.pair, self.x_out, self.keep, self.x_in, self.z_out, self.z_in, self.full = bufs
         self.send, self.recv = send, recv
-        self.half = self.pair.shape[0]
-        self.quarter = self.half // 2
         n_hi = at["n_hi"]
-        self.size = self.quarter // n_hi
+        self.half = self.part.shape[0] // 2
+        self.size = self.half // n_hi
         self.subs = subs_of(self.size)
+        self.step = self.size // self.subs
         self.bits = [1 << b for b in reversed(range(n_hi.bit_length() - 1))]
         self.masks = sorted(range(1, n_hi), key=lambda m: (-(m & -m), m))
+        self.order = list(range(1, n_hi)) + [0]
         self.base = recv_layout(n_hi, self.subs)[0]
 
     def rows(self, start, size):
         return pl.ds(pl.multiple_of(start, math.gcd(size, 128)), size)
 
     def place(self, lo, hi, sub=None):
-        start = self.at["par"] * self.half + lo * self.quarter + hi * self.size
+        start = lo * self.half + hi * self.size
         if sub is None:
             return self.rows(start, self.size)
-        step = self.size // self.subs
-        return self.rows(start + sub * step, step)
+        return self.rows(start + sub * self.step, self.step)
 
     def go(self, src, dst, stage, k, dp):
-        one = self.copy(src, dst, self.send.at[stage], self.recv.at[self.base[stage] + k], dp, self.at["emb"])
-        one.start()
-        return one
-
-    def start(self, away):
-        lo = 1 - self.at["low"] if away else self.at["low"]
-        src = self.rows((1 - self.at["par"]) * self.half + lo * self.quarter, self.quarter)
-        dst = self.rows(lo * self.quarter, self.quarter)
-        one = self.go(self.part.at[src], self.pair.at[dst], 0, 0 if away else 1, self.at["partner"])
-        if away:
-            self.first_away = one
-        else:
-            self.first_keep = one
-
-    def stage_x(self):
+        self.copy(src, dst, self.send.at[stage], self.recv.at[self.base[stage] + k], dp, self.at["emb"]).start()
+
+    def waiter(self, ref, stage, k=0):
+        return self.copy(
+            ref, ref, self.send.at[stage], self.recv.at[self.base[stage] + k], self.at["partner"], self.at["emb"]
+        )
+
+    def got(self, ref, stage, k):
+        self.waiter(ref, stage, k).wait_recv()
+
+    def start(self, k):
         at = self.at
-        self.first_away.wait_recv()
-        self.x, self.z = {}, {}
-        lo = (1 - at["low"]) * self.quarter
-        for k in list(range(1, at["n_hi"])) + [0]:
-            piece = at["ahead"][k] * self.size
-            mine = self.part[self.rows(at["par"] * self.half + lo + piece, self.size), :]
-            theirs = self.pair[self.rows(lo + piece, self.size), :]
-            self.x_out[k] = (mine.astype(F32) + theirs.astype(F32)).astype(BF16)
-            self.x[k] = self.go(self.x_out.at[k], self.x_in.at[k], 1, k, at["beside"])
+        piece = self.place(1 - at["low"], at["ahead"][k])
+        self.go(self.part.at[piece], self.pair.at[piece], 0, k, at["partner"])
+
+    def start_keep(self):
+        at = self.at
+        kept = self.rows(at["low"] * self.half, self.half)
+        self.go(self.part.at[kept], self.pair.at[kept], 0, at["n_hi"], at["partner"])
+
+    def stage_x(self, k):
+        at = self.at
+        self.got(self.pair.at[0 : self.size], 0, k)
+        piece = self.place(1 - at["low"], at["ahead"][k])
+        both = self.part[piece, :].astype(F32) + self.pair[piece, :].astype(F32)
+        self.x_out[k] = both.astype(BF16)
+        self.go(self.x_out.at[k], self.x_in.at[k], 1, k, at["beside"])
 
     def stage_keep(self):
         at = self.at
-        self.first_keep.wait_recv()
-        lo = at["low"] * self.quarter
-        mine = self.part[self.rows(at["par"] * self.half + lo, self.quarter), :]
-        theirs = self.pair[self.rows(lo, self.quarter), :]
-        self.keep[...] = mine.astype(F32) + theirs.astype(F32)
+        self.got(self.pair.at[0 : self.half], 0, at["n_hi"])
+        kept = self.rows(at["low"] * self.half, self.half)
+        self.keep[...] = self.part[kept, :].astype(F32) + self.pair[kept, :].astype(F32)
 
     def joined(self, k):
-        self.x[k].wait_recv()
+        self.got(self.x_in.at[k], 1, k)
         kept = self.keep[self.rows(self.at["ahead"][k] * self.size, self.size), :]
         return kept + self.x_in[k].astype(F32)
 
     def stage_z(self, k):
         self.z_out[k - 1] = self.joined(k).astype(BF16)
-        self.z[k] = self.go(
-            self.z_out.at[k - 1], self.z_in.at[k - 1], 2, k - 1, self.at["far"][k]
-        )
+        self.go(self.z_out.at[k - 1], self.z_in.at[k - 1], 2, k - 1, self.at["far"][k])
 
     def stage_sum(self):
         at = self.at
         total = self.joined(0)
         for k in range(1, at["n_hi"]):
-            self.z[k].wait_recv()
+            self.got(self.z_in.at[k - 1], 2, k - 1)
             total = total + self.z_in[k - 1].astype(F32)
         self.full[self.place(at["low"], at["high"]), :] = total.astype(BF16)
-        self.far, self.near = {}, {}
         for bit in self.bits:
             for sub in range(self.subs):
                 self.pass_on(0, sub, bit)
@@ -112,25 +109,24 @@
     def pass_on(self, mask, sub, bit):
         at = self.at
         view = self.full.at[self.place(at["low"], flip(at["high"], mask), sub)]
-        got = mask | bit
         peer = (2 * flip(at["high"], bit) + at["low"]) * 2 + at["par"]
-        self.far[got, sub] = self.go(view, view, 3, self.masks.index(got) * self.subs + sub, peer)
+        self.go(view, view, 3, self.masks.index(mask | bit) * self.subs + sub, peer)
 
     def pass_near(self, mask, sub):
         at = self.at
         view = self.full.at[self.place(at["low"], flip(at["high"], mask), sub)]
-        self.near[mask, sub] = self.go(view, view, 4, mask * self.subs + sub, at["beside"])
+        self.go(view, view, 4, mask * self.subs + sub, at["beside"])
         self.go(view, view, 5, 0, at["partner"])
 
     def take_far(self, mask, sub):
-        self.far[mask, sub].wait_recv()
+        self.got(self.full.at[0 : self.step], 3, self.masks.index(mask) * self.subs + sub)
         for bit in self.bits:
             if bit < (mask & -mask):
                 self.pass_on(mask, sub, bit)
         self.pass_near(mask, sub)
 
     def take_near(self, mask, sub):
-        self.near[mask, sub].wait_recv()
+        self.got(self.full.at[0 : self.step], 4, mask * self.subs + sub)
         view = self.full.at[self.place(1 - self.at["low"], flip(self.at["high"], mask), sub)]
         self.go(view, view, 5, 0, self.at["partner"])
 
@@ -144,20 +140,16 @@
         for item in near[len(far) - self.subs :]:
             self.take_near(*item)
 
-    def finish(self):
-        partner = self.at["partner"]
-
-        def sizes(ref, stage, k=0):
-            return self.copy(ref, ref, self.send.at[stage], self.recv.at[self.base[stage] + k], partner, self.at["emb"])
-
-        whole = self.full.at[self.rows((1 - self.at["par"]) * self.half, self.half)]
-        sizes(whole, 5).wait_recv()
-        sizes(self.pair, 0).wait_send()
-        sizes(self.x_out, 1).wait_send()
-        sizes(self.z_out, 2).wait_send()
-        sizes(self.z_out, 3).wait_send()
-        sizes(self.x_out, 4).wait_send()
-        sizes(whole, 5).wait_send()
+    def finish_owner(self):
+        self.waiter(self.x_out, 1).wait_send()
+        self.waiter(self.z_out, 2).wait_send()
+        self.waiter(self.z_out, 3).wait_send()
+        self.waiter(self.x_out, 4).wait_send()
+        self.waiter(self.full, 5).wait_send()
+
+    def finish_other(self):
+        self.waiter(self.pair, 0).wait_send()
+        self.got(self.full, 5, 0)
 
 
 def flip(index, mask):
@@ -174,7 +166,7 @@
 
 
 def recv_layout(n_hi, subs):
-    counts = [2, n_hi, n_hi - 1, (n_hi - 1) * subs, n_hi * subs, 1]
+    counts = [n_hi + 1, n_hi, n_hi - 1, (n_hi - 1) * subs, n_hi * subs, 1]
     starts = [sum(counts[:i]) for i in range(len(counts))]
     return starts, sum(counts)
 
@@ -374,18 +366,16 @@
             grad_copies = to_peers(own_grads, lambda k: own_grads)
         prev_pos.append((e, place_of(ids[e, 1]) - base))
 
-    half_rows = rows // 2
-    pt = 128 if half_rows % 128 == 0 else half_rows
-
-    def grad_half(which):
-        for i in range(half_rows // pt):
-            at_row = pl.multiple_of(which * half_rows + i * pt, pt)
-            index = lax.broadcasted_iota(jnp.int32, (pt, tok), 0) + at_row
+    pt = 128 if rows % 128 == 0 else rows
+
+    def table_sums():
+        for i in range(rows // pt):
+            index = lax.broadcasted_iota(jnp.int32, (pt, tok), 0) + i * pt
             acc = jnp.zeros((pt, LANES), F32)
             for e, pos in prev_pos:
                 hot = jnp.where(index == pos, 1.0, 0.0).astype(BF16)
                 acc = acc + dot(hot, gall[e])
-            tpart[pl.ds(at_row, pt), :] = acc
+            tpart[i * pt : (i + 1) * pt, :] = acc
 
     for one in loads[5:]:
         one.wait()
@@ -435,12 +425,19 @@
         if q == 1:
             for one in grad_copies:
                 one.wait_recv()
-            grad_half(1 - par)
-            sums.start(True)
-            sums.start(False)
-            grad_half(par)
-    sums.stage_x()
-    sums.stage_keep()
+            table_sums()
+
+            @pl.when(par == 1)
+            def _():
+                for k in sums.order:
+                    sums.start(k)
+                sums.start_keep()
+
+    @pl.when(par == 0)
+    def _():
+        for k in sums.order:
+            sums.stage_x(k)
+        sums.stage_keep()
 
     for one in logit_copies:
         one.wait_recv()
@@ -453,70 +450,111 @@
         span = slice(e * tok, (e + 1) * tok)
         lead[:, span] = (normed_t[:, span] * slope).astype(BF16)
 
-    def weight_grads(which, lo):
-        factor = scale * (0.5 + 0.5 * which.astype(F32))
-        for i in range(tiles // 2):
-            j = lo * (tiles // 2) + i
-            cols = pl.ds(pl.multiple_of(j * ht, ht), ht)
-            part = (dot(lead[...], act[which, :, cols]) * (head_of(j) * factor)).astype(BF16)
-            for b in range(per_tile):
-                to = which * hid + j * ht + b * LANES
-                gpart[pl.ds(pl.multiple_of(to, LANES), LANES), :] = part[:, b * LANES : (b + 1) * LANES]
-
-    weight_grads(1 - par, 1 - low)
-    tower.start(True)
-    weight_grads(par, 1 - low)
-    tower.stage_x()
-    for k in range(1, n_hi):
-        sums.stage_z(k)
-    weight_grads(1 - par, low)
-    tower.start(False)
-    weight_grads(par, low)
-    tower.stage_keep()
-    tower.stage_z(1)
-    sums.stage_sum()
-    for k in range(2, n_hi):
-        tower.stage_z(k)
-
-    for j in range(tiles):
-        cols = slice(j * ht, (j + 1) * ht)
-        head = head_of(j)
-        scaled_w[0, :, cols] = (wg[:, cols].astype(F32) * (0.5 * head)).astype(BF16)
-        scaled_w[1, :, cols] = (wu[:, cols].astype(F32) * head).astype(BF16)
-    back_copies = []
-    for q in range(1, n_emb + 1):
-        e = other_emb(n_emb - q)
-        span = tokens(e)
-        bn[span, :] = dot_nt(act[0, span, :], scaled_w[0]) + dot_nt(act[1, span, :], scaled_w[1])
-        if q < n_emb:
-            back_copies += to_peers(bn.at[span], lambda k: bn_in.at[k - 1], [n_emb - q])
-
-    for mask in sums.masks:
-        sums.take_far(mask, 0)
-    tower.stage_sum()
-    sums.take_near(0, 0)
-    for mask in sums.masks:
-        sums.take_near(mask, 0)
-
-    for one in back_copies:
-        one.wait_recv()
-    own = tokens(me_emb)
-    back = bn[own, :]
-    for k in range(n_emb - 1):
-        back = back + bn_in[k]
-    slope_col = jnp.broadcast_to(slopes[me_emb], (LANES, tok)).T
-    scaled = back * slope_col * gain[...]
-    x = values[own, :]
-    inv = lax.rsqrt(jnp.mean(x * x, axis=1, keepdims=True) + norm_eps)
-    emb_ref[...] = inv * scaled - x * (inv * inv * inv) * jnp.mean(
-        x * scaled, axis=1, keepdims=True
-    )
-
-    tower.spread()
-    sums.finish()
-    total_ref[...] = tall[...]
-    tower.finish()
-    tower_ref[...] = gall_sum[...]
+    def weight_block(which, col, width, to):
+        factor = scale * (0.5 + 0.5 * which)
+        heads = [wo_row[pl.ds(col // LANES + b, 1), :] for b in range(width // LANES)]
+        head = jnp.concatenate(heads, axis=1) * factor
+        cols = pl.ds(pl.multiple_of(col, width), width)
+        part = (dot(lead[...], act[which, :, cols]) * head).astype(BF16)
+        for b in range(width // LANES):
+            gpart[pl.ds(pl.multiple_of(to + b * LANES, LANES), LANES), :] = part[
+                :, b * LANES : (b + 1) * LANES
+            ]
+
+    side = hid // 2
+
+    def weight_side(lo):
+        width = min(ht, side)
+        for which in range(2):
+            for i in range(side // width):
+                weight_block(which, lo * side + i * width, width, lo * hid + which * side + i * width)
+
+    by_piece = tower.size % LANES == 0 and side % tower.size == 0
+
+    def weight_piece(k):
+        if not by_piece:
+            if k == tower.order[0]:
+                weight_side(1 - low)
+            return
+        width = min(ht, tower.size)
+        first = at["ahead"][k] * tower.size
+        which = first // side
+        for i in range(tower.size // width):
+            col = (1 - low) * side + first % side + i * width
+            weight_block(which, col, width, (1 - low) * hid + first + i * width)
+
+    back_slot = len(pending)
+
+    def back_copy(k):
+        span = tokens(other_emb(k))
+        slot = back_slot + k - 1
+        return copy(bn.at[span], bn_in.at[k - 1], e_send.at[slot], e_recv.at[slot], me_dp, other_emb(k))
+
+    def backward():
+        for j in range(tiles):
+            cols = slice(j * ht, (j + 1) * ht)
+            head = head_of(j)
+            scaled_w[0, :, cols] = (wg[:, cols].astype(F32) * (0.5 * head)).astype(BF16)
+            scaled_w[1, :, cols] = (wu[:, cols].astype(F32) * head).astype(BF16)
+        for k in range(n_emb - 1, -1, -1):
+            span = tokens(other_emb(k))
+            bn[span, :] = dot_nt(act[0, span, :], scaled_w[0]) + dot_nt(act[1, span, :], scaled_w[1])
+            if k > 0:
+                back_copy(k).start()
+
+    def embed():
+        for k in range(1, n_emb):
+            back_copy(k).wait()
+        own = tokens(me_emb)
+        back = bn[own, :]
+        for k in range(n_emb - 1):
+            back = back + bn_in[k]
+        slope_col = jnp.broadcast_to(slopes[me_emb], (LANES, tok)).T
+        scaled = back * slope_col * gain[...]
+        x = values[own, :]
+        inv = lax.rsqrt(jnp.mean(x * x, axis=1, keepdims=True) + norm_eps)
+        emb_ref[...] = inv * scaled - x * (inv * inv * inv) * jnp.mean(
+            x * scaled, axis=1, keepdims=True
+        )
+
+    @pl.when(par == 1)
+    def _():
+        for i, k in enumerate(tower.order):
+            weight_piece(k)
+            if i > 0:
+                tower.stage_x(tower.order[i - 1])
+        tower.stage_x(tower.order[-1])
+        weight_side(low)
+        tower.stage_keep()
+        for k in range(1, n_hi):
+            tower.stage_z(k)
+        backward()
+        tower.stage_sum()
+        embed()
+        tower.spread()
+        tower_ref[...] = gall_sum[...]
+        sums.finish_other()
+        total_ref[...] = tall[...]
+        tower.finish_owner()
+
+    @pl.when(par == 0)
+    def _():
+        for k in tower.order:
+            weight_piece(k)
+            tower.start(k)
+        weight_side(low)
+        tower.start_keep()
+        for k in range(1, n_hi):
+            sums.stage_z(k)
+        backward()
+        sums.stage_sum()
+        embed()
+        sums.spread()
+        total_ref[...] = tall[...]
+        sums.finish_owner()
+        tower.finish_other()
+        tower_ref[...] = gall_sum[...]
+
     for one in pending:
         one.wait_send()
 
@@ -540,7 +578,8 @@
     for which, (buf, out) in enumerate(((gate, gate_out), (up, up_out))):
         for c in range(n_col):
             for b in range(c * hid // LANES // n_col, (c + 1) * hid // LANES // n_col):
-                start = which * hid + b * LANES
+                half_blocks = hid // LANES // 2
+                start = (b // half_blocks) * hid + which * (hid // 2) + b % half_blocks * LANES
                 buf[:, b * LANES : (b + 1) * LANES] = tower_ref[start : start + LANES, :].astype(F32)
             cols = slice(c * hid // n_col, (c + 1) * hid // n_col)
             send(buf.at[:, cols], out.at[:, cols])
@@ -579,12 +618,12 @@
 
     def reduce_buffers(total_rows, dtype):
         half = total_rows // 2
-        size = half // n_chip
+        size = half // n_hi
         return [
             pltpu.VMEM((total_rows, width), dtype),
-            pltpu.VMEM((half, width), dtype),
+            pltpu.VMEM((total_rows, width), dtype),
             pltpu.VMEM((n_hi, size, width), BF16),
-            pltpu.VMEM((half // 2, width), F32),
+            pltpu.VMEM((half, width), F32),
             pltpu.VMEM((n_hi, size, width), BF16),
             pltpu.VMEM((n_hi - 1, size, width), BF16),
             pltpu.VMEM((n_hi - 1, size, width), BF16),
@@ -633,9 +672,9 @@
             dma((emb_copies,)),
             dma((emb_copies,)),
             dma((6,)),
-            dma((recv_layout(n_hi, subs_of(rows // 4 // n_hi))[1],)),
+            dma((recv_layout(n_hi, subs_of(rows // 2 // n_hi))[1],)),
             dma((6,)),
-            dma((recv_layout(n_hi, subs_of(hid // 2 // n_hi))[1],)),
+            dma((recv_layout(n_hi, subs_of(hid // n_hi))[1],)),
         ],
         compiler_params=pltpu.CompilerParams(
             collective_id=0, has_side_effects=True, vmem_limit_bytes=40 * 1024 * 1024

time: 43.4 us -> 42.2 us (0.972)
  Pallas kernels: 42.5 us -> 41.4 us
    pallas_call x1, Pallas kernels: 40.6 us -> 39.5 us  [on_device(): pl.pallas_call(functools.partial(tower_kernel, n_dp, n_emb, scale), out_s...]
where the time goes in v4:
time: 42.2 us; the launch traced here: 42.1 us
  Pallas kernels  41.4 us (98%)
  between operations  0.68 us (2%)
    pallas_call x1, Pallas kernels, on_device(): pl.pallas_call(functools.partial(tower_kernel, n_dp, n_emb, scale), out_s...  39.5 us
    pallas_call x1, Pallas kernels, on_device(): pl.pallas_call(write_kernel, out_shape=(jax.ShapeDtypeStruct((rows, width...  1.96 us

profile of v4, /device:TPU:0, one launch (start us, length us, event | category | flops | bytes accessed | tf_op | source)
XLA Modules:
  0.0 42.1 jit_solution(10324874783265895774)
XLA Ops:
  0.6 0.0 copy-start
  0.6 0.0 copy-start.1
  0.7 39.5 %shard_map.146 = (bf16[1536,128]{1,0:T(8,128)(2,1)S(1)}, bf16[4096,128]{1,0:T(8,128)(2,1)S(1)}, f32[256,128]{1,0:T(8,128)S(1)}) custom-call(s32[1,256]{1,0:T(1,128)} %bitcast.9, s32[1,256]{1,0:T(1,128)} %bitcast.10, bf16[256,128]{1,0:T(8,128)(2,1)} %grads_ref.1, s32[24,128]{1,0:T(8,128)} %bitcast.6, f32[1536,128]{1,0:T(8,128)} %table_ref.3, ...), custom_call_target="tpu_custom_call" | custom-call | tf_op jit(solution)/shard_map/pallas_call | solution.py:633
  40.1 0.0 copy-done
  40.1 0.0 copy-done.1
  40.1 2.0 %shard_map.147 = (f32[1536,128]{1,0:T(8,128)}, f32[1536,128]{1,0:T(8,128)}, f32[128,2048]{1,0:T(8,128)}, f32[128,2048]{1,0:T(8,128)}, f32[256,128]{1,0:T(8,128)}) custom-call(bf16[1536,128]{1,0:T(8,128)(2,1)S(1)} %get-tuple-element.8.total_ref, f32[1536,128]{1,0:T(8,128)S(1)} %copy-done, f32[1536,128]{1,0:T(8,128)S(1)} %copy-done.1, ...), custom_call_target="tpu_custom_call" | custom-call | tf_op jit(solution)/shard_map/pallas_call | solution.py:699
Async XLA Ops:
  0.6 39.5 %copy-start = (f32[1536,128]{1,0:T(8,128)S(1)}, f32[1536,128]{1,0:T(8,128)}, u32[]{:S(2)}) copy-start(f32[1536,128]{1,0:T(8,128)} %table_ref.3) | copy-start | bytes 2359300
  0.6 39.5 %copy-start.1 = (f32[1536,128]{1,0:T(8,128)S(1)}, f32[1536,128]{1,0:T(8,128)}, u32[]{:S(2)}) copy-start(f32[1536,128]{1,0:T(8,128)} %accum_ref.1) | copy-start | bytes 2359300

commit v5 on v4

--- a/solution.py
+++ b/solution.py
@@ -162,7 +162,7 @@
 
 
 def subs_of(size):
-    return 4 if size % 256 == 0 else 1
+    return 8 if size % 256 == 0 else 1
 
 
 def recv_layout(n_hi, subs):
@@ -323,6 +323,9 @@
 
     own_ids = ids.at[me_emb]
     id_copies = to_peers(own_ids, lambda k: own_ids)
+    loads[3].wait()
+    own_grads = gall.at[me_emb]
+    grad_copies = to_peers(own_grads, lambda k: own_grads)
     loads[2].wait()
     groups = place.shape[0]
     stored = place[...]
@@ -360,22 +363,35 @@
         contrib[tokens(e), :] = acc.astype(BF16)
         for k, one in enumerate(to_peers(view, lambda k: lbuf.at[k - 1, tokens(e)])):
             row_copies[k + 1, s] = one
-        if s == 0:
-            loads[3].wait()
-            own_grads = gall.at[me_emb]
-            grad_copies = to_peers(own_grads, lambda k: own_grads)
         prev_pos.append((e, place_of(ids[e, 1]) - base))
 
-    pt = 128 if rows % 128 == 0 else rows
-
-    def table_sums():
-        for i in range(rows // pt):
-            index = lax.broadcasted_iota(jnp.int32, (pt, tok), 0) + i * pt
+    half_rows = rows // 2
+    pt = 128 if half_rows % 128 == 0 else half_rows
+
+    def table_sums(lo):
+        for i in range(half_rows // pt):
+            at_row = pl.multiple_of(lo * half_rows + i * pt, pt)
+            index = lax.broadcasted_iota(jnp.int32, (pt, tok), 0) + at_row
             acc = jnp.zeros((pt, LANES), F32)
             for e, pos in prev_pos:
                 hot = jnp.where(index == pos, 1.0, 0.0).astype(BF16)
                 acc = acc + dot(hot, gall[e])
-            tpart[i * pt : (i + 1) * pt, :] = acc
+            tpart[pl.ds(at_row, pt), :] = acc.astype(BF16)
+
+    for one in grad_copies:
+        one.wait_recv()
+    table_sums(1 - low)
+
+    @pl.when(par == 1)
+    def _():
+        for k in sums.order:
+            sums.start(k)
+
+    table_sums(low)
+
+    @pl.when(par == 1)
+    def _():
+        sums.start_keep()
 
     for one in loads[5:]:
         one.wait()
@@ -423,20 +439,14 @@
         view = logit.at[e]
         logit_copies += to_peers(view, lambda k: logit_in.at[k - 1, e])
         if q == 1:
-            for one in grad_copies:
-                one.wait_recv()
-            table_sums()
-
-            @pl.when(par == 1)
+
+            @pl.when(par == 0)
             def _():
                 for k in sums.order:
-                    sums.start(k)
-                sums.start_keep()
+                    sums.stage_x(k)
 
     @pl.when(par == 0)
     def _():
-        for k in sums.order:
-            sums.stage_x(k)
         sums.stage_keep()
 
     for one in logit_copies:
@@ -542,10 +552,10 @@
         for k in tower.order:
             weight_piece(k)
             tower.start(k)
+        for k in range(1, n_hi):
+            sums.stage_z(k)
         weight_side(low)
         tower.start_keep()
-        for k in range(1, n_hi):
-            sums.stage_z(k)
         backward()
         sums.stage_sum()
         embed()
@@ -665,7 +675,7 @@
             pltpu.VMEM((group, width), F32),
             pltpu.VMEM((n_peer, tok, width), F32),
         ]
-        + reduce_buffers(rows, F32)
+        + reduce_buffers(rows, BF16)
         + reduce_buffers(2 * hid, BF16)
         + [
             dma((10,)),

time: 42.2 us -> 41.8 us (level)
  no operation moved by 1% of the time
where the time goes in v5:
time: 41.8 us; the launch traced here: 41.7 us
  Pallas kernels  41 us (98%)
  between operations  0.68 us (2%)
    pallas_call x1, Pallas kernels, on_device(): pl.pallas_call(functools.partial(tower_kernel, n_dp, n_emb, scale), out_s...  39 us
    pallas_call x1, Pallas kernels, on_device(): pl.pallas_call(write_kernel, out_shape=(jax.ShapeDtypeStruct((rows, width...  1.96 us

profile of v5, /device:TPU:0, one launch (start us, length us, event | category | flops | bytes accessed | tf_op | source)
XLA Modules:
  0.0 41.7 jit_solution(5867242248480311704)
XLA Ops:
  0.6 0.0 copy-start
  0.6 0.0 copy-start.1
  0.7 39.0 %shard_map.146 = (bf16[1536,128]{1,0:T(8,128)(2,1)S(1)}, bf16[4096,128]{1,0:T(8,128)(2,1)S(1)}, f32[256,128]{1,0:T(8,128)S(1)}) custom-call(s32[1,256]{1,0:T(1,128)} %bitcast.9, s32[1,256]{1,0:T(1,128)} %bitcast.10, bf16[256,128]{1,0:T(8,128)(2,1)} %grads_ref.1, s32[24,128]{1,0:T(8,128)} %bitcast.6, f32[1536,128]{1,0:T(8,128)} %table_ref.3, ...), custom_call_target="tpu_custom_call" | custom-call | tf_op jit(solution)/shard_map/pallas_call | solution.py:643
  39.7 0.0 copy-done
  39.7 0.0 copy-done.1
  39.7 2.0 %shard_map.147 = (f32[1536,128]{1,0:T(8,128)}, f32[1536,128]{1,0:T(8,128)}, f32[128,2048]{1,0:T(8,128)}, f32[128,2048]{1,0:T(8,128)}, f32[256,128]{1,0:T(8,128)}) custom-call(bf16[1536,128]{1,0:T(8,128)(2,1)S(1)} %get-tuple-element.8.total_ref, f32[1536,128]{1,0:T(8,128)S(1)} %copy-done, f32[1536,128]{1,0:T(8,128)S(1)} %copy-done.1, ...), custom_call_target="tpu_custom_call" | custom-call | tf_op jit(solution)/shard_map/pallas_call | solution.py:709
Async XLA Ops:
  0.6 39.1 %copy-start = (f32[1536,128]{1,0:T(8,128)S(1)}, f32[1536,128]{1,0:T(8,128)}, u32[]{:S(2)}) copy-start(f32[1536,128]{1,0:T(8,128)} %table_ref.3) | copy-start | bytes 2359300
  0.6 39.1 %copy-start.1 = (f32[1536,128]{1,0:T(8,128)S(1)}, f32[1536,128]{1,0:T(8,128)}, u32[]{:S(2)}) copy-start(f32[1536,128]{1,0:T(8,128)} %accum_ref.1) | copy-start | bytes 2359300
